TPU v7x, 256 devices: a whole 4x4x8 slice. The times are simulated.
256 devices in a mesh: gz: 16 (over z, y_lo), pa: 16 (over y_hi, x, core).
Axes of the slice: x: 4, y: 4 (y_hi: 2, y_lo: 2; y = y_hi * 2 + y_lo), z: 8, core: 2. Of those that a mesh axis runs over, the one named last changes fastest.
Arguments:
- density: bfloat16 [64, 1024, 1024], P('gz', 'pa'), may hold values from -6 to 6
- green: float32 [128, 1024, 1024], P('gz', 'pa'), may hold values from 0.1 to 3
Outputs:
- potential: float32 [64, 1024, 1024], P('gz', 'pa')
All inputs are finite; a program needn't handle non-finite values.
Results may differ from a plain program's by a relative error of at most 0.02.
Values may be sent and summed in bfloat16 or wider, within the bound.
No kernel may reach another device: no remote copies, remote signals or barrier semaphores. Data moves between devices by JAX's collectives and lax.ppermute only.
A program may use at most 64 MiB of HBM per device.

v0:
```python
import math

import jax
import jax.numpy as jnp
from jax import lax
from jax.experimental import pallas as pl
from jax.experimental.pallas import tpu as pltpu
from jax.sharding import PartitionSpec as P


F32, BF16 = jnp.float32, jnp.bfloat16
LANES = 128
VMEM = pl.BlockSpec(memory_space=pltpu.VMEM)
SMEM = pl.BlockSpec(memory_space=pltpu.SMEM)
ANY = pl.BlockSpec(memory_space=pl.ANY)


def call(kernel, outs, *args, specs=None, inside=(), keep=False, limit=24, **kwargs):
    args = [pltpu.with_memory_space_constraint(a, pltpu.VMEM) if i in inside else a for i, a in enumerate(args)]
    out_specs = jax.tree.map(lambda _: VMEM, outs)
    if keep:
        outs = jax.tree.map(lambda o: pltpu.VMEM(o.shape, o.dtype), outs)
    return pl.pallas_call(
        kernel,
        out_shape=outs,
        in_specs=specs or [VMEM] * len(args),
        out_specs=out_specs,
        compiler_params=pltpu.CompilerParams(vmem_limit_bytes=limit * 2**20),
        **kwargs,
    )(*args)


def fetch(table_ref, buffer, sem):
    copy = pltpu.make_async_copy(table_ref, buffer, sem)
    copy.start()
    return copy


def array(*shape, dtype=BF16):
    return jax.ShapeDtypeStruct(shape, dtype)


def trig(product, length):
    angle = (product % length).astype(F32) * (2.0 * math.pi / length)
    return jnp.cos(angle), jnp.sin(angle)


def cas_square(length, fine=32):
    k = jnp.arange(length, dtype=jnp.int32)[None, :]
    ca, sa = trig(jnp.arange(length // fine, dtype=jnp.int32)[:, None] * fine * k, length)
    cb, sb = trig(jnp.arange(fine, dtype=jnp.int32)[:, None] * k, length)
    ca, sa, plus, minus = lax.optimization_barrier((ca, sa, cb + sb, cb - sb))
    table = ca[:, None, :] * plus[None] + sa[:, None, :] * minus[None]
    return lax.optimization_barrier(table.reshape(length, length).astype(BF16))


def swap_halves(first, second, axis):
    half = first.shape[axis] // 2
    lower = lax.broadcasted_iota(jnp.int32, first.shape, axis) < half
    return (
        jnp.where(lower, first, pltpu.roll(second, half, axis)),
        jnp.where(lower, pltpu.roll(first, half, axis), second),
    )


def convert_kernel(me_ref, green_ref, *refs):
    *out_refs, buffer, sems = refs
    copies = []
    for s in range(len(out_refs)):
        at = pl.multiple_of(jnp.bitwise_xor(me_ref[0] // 2, s) * 8, 8)
        copies.append(pltpu.make_async_copy(green_ref.at[:, pl.ds(at, 8), :], buffer.at[s], sems.at[s]))
        copies[-1].start()
    for s, out_ref in enumerate(out_refs):
        copies[s].wait()
        out_ref[...] = buffer[s].reshape(out_ref.shape).astype(BF16)


def share_kernel(me_ref, *refs):
    *in_refs, keep_ref, send_ref = refs
    flip = me_ref[0] % 2
    shape = keep_ref.shape[1:]
    for s, in_ref in enumerate(in_refs):
        block = in_ref[...].astype(F32).reshape(in_ref.shape[0] // 16, 2, 8, in_ref.shape[1])
        low, high = swap_halves(block[:, 0], block[:, 1], 1)
        keep_ref[s] = jnp.where(flip == 0, low, high).reshape(shape).astype(BF16)
        send_ref[s] = jnp.where(flip == 0, high, low).reshape(shape).astype(BF16)


def expand_kernel(table_ref, forth_ref, back_ref, *, v_sub):
    small = table_ref[...]
    freqs, cells = small.shape
    rows, cols = forth_ref.shape
    half = cols // 2

    def iota(shape, axis):
        return lax.broadcasted_iota(jnp.int32, shape, axis)

    def z_of(c):
        return c % half // 8 * 4 + c // v_sub % 2 * 2 + c // half

    def ones(mask):
        return jnp.where(mask, 1.0, 0.0).astype(BF16)

    spread = ones(iota((rows, freqs), 0) // v_sub == iota((rows, freqs), 1))
    pick = ones(iota((cells, cols), 0) == z_of(iota((cells, cols), 1)))
    full = jnp.dot(jnp.dot(spread, small, preferred_element_type=F32).astype(BF16), pick, preferred_element_type=F32)
    same = iota((rows, cols), 0) % v_sub == iota((rows, cols), 1) % v_sub
    forth_ref[...] = jnp.where(same, full, 0.0).astype(BF16)
    pick = ones(z_of(iota((cols, cells), 0)) == iota((cols, cells), 1))
    spread = ones(iota((freqs, rows), 1) // v_sub == iota((freqs, rows), 0))
    part = lax.dot_general(pick, small, (((1,), (1,)), ((), ())), preferred_element_type=F32).astype(BF16)
    full = jnp.dot(part, spread, preferred_element_type=F32)
    same = iota((cols, rows), 0) % v_sub == iota((cols, rows), 1) % v_sub
    back_ref[...] = jnp.where(same, full, 0.0).astype(BF16)


def forward_kernel(density_ref, table_ref, out_ref):
    spec = lax.dot_general(table_ref[...], density_ref[...], (((1,), (1,)), ((), ())), preferred_element_type=F32)
    tiles = spec.shape[0] // 8
    left = spec[:, :LANES].reshape(tiles, 8, LANES)
    right = spec[:, LANES:].reshape(tiles, 8, LANES)
    even, odd = swap_halves(left, right, 1)
    out_ref[:, 0] = even.astype(BF16)
    out_ref[:, 1] = odd.astype(BF16)


def spectrum_kernel(moved_ref, table_ref, out_ref, buffer, sem):
    copy = fetch(table_ref, buffer, sem)
    pencils, groups = moved_ref.shape[:2]
    rows = groups * 8
    low, high = [], []
    for q in range(pencils // 2):
        left = moved_ref[2 * q].reshape(rows, LANES).astype(F32)
        right = moved_ref[2 * q + 1].reshape(rows, LANES).astype(F32)
        a, b = swap_halves(left, right, 1)
        low.append(a.astype(BF16))
        high.append(b.astype(BF16))
    data = jnp.concatenate([jnp.concatenate(low, axis=1), jnp.concatenate(high, axis=1)], axis=0)
    copy.wait()
    out_ref[...] = jnp.dot(data, buffer[...], preferred_element_type=F32).astype(BF16)


def solve_kernel(spec_ref, forth_ref, back_ref, table_ref, keep_ref, came_ref, out_ref, buffer, sem):
    copy = fetch(table_ref, buffer, sem)
    zspec = jnp.dot(forth_ref[...], spec_ref[...], preferred_element_type=F32)
    rows = zspec.shape[0] // 2
    shape = (rows, zspec.shape[1])
    weighted = jnp.concatenate(
        [
            (zspec[:rows] * keep_ref[...].reshape(shape).astype(F32)).astype(BF16),
            (zspec[rows:] * came_ref[...].reshape(shape).astype(F32)).astype(BF16),
        ],
        axis=0,
    )
    total = jnp.dot(back_ref[...], weighted, preferred_element_type=F32).astype(BF16)
    copy.wait()
    values = jnp.dot(total, buffer[...], preferred_element_type=F32)
    half = values.shape[0] // 2
    shape = out_ref.shape[1:]
    for q in range(out_ref.shape[0] // 2):
        at = slice(q * LANES, (q + 1) * LANES)
        a, b = swap_halves(values[:half, at], values[half:, at], 1)
        out_ref[2 * q] = a.astype(BF16).reshape(shape)
        out_ref[2 * q + 1] = b.astype(BF16).reshape(shape)


def inverse_kernel(came_ref, table_ref, out_ref, buffer, sem, *, scale):
    copy = fetch(table_ref, buffer, sem)
    even = came_ref[:, 0].astype(F32)
    odd = came_ref[:, 1].astype(F32)
    left, right = swap_halves(even, odd, 1)
    rows = left.shape[0] * 8
    data = jnp.concatenate([left.reshape(rows, LANES), right.reshape(rows, LANES)], axis=1).astype(BF16)
    copy.wait()
    out = lax.dot_general(data, buffer[...], (((0,), (0,)), ((), ())), preferred_element_type=F32)
    out_ref[...] = out * scale


def local(density, green):
    z_slab, x_local, y_cells = density.shape
    k_block, y_local, x_cells = green.shape
    groups = lax.axis_size("gz")
    pencils = lax.axis_size("pa")
    v_sub = y_local // groups
    z_cells = z_slab * groups
    z_freqs = k_block * groups
    lines = z_slab * x_local
    steps = groups // 2
    me = lax.axis_index("gz").astype(jnp.int32)
    place = me.reshape(1)

    pieces = call(
        convert_kernel,
        (array(k_block * 2 * v_sub, x_cells),) * steps,
        place,
        green,
        specs=[SMEM, ANY],
        scratch_shapes=[pltpu.VMEM((steps, k_block, 2 * v_sub, x_cells), F32), pltpu.SemaphoreType.DMA((steps,))],
    )
    pieces = list(pieces)
    for s in range(1, steps):
        pieces[s] = lax.ppermute(pieces[s], "gz", [(i, i ^ 2 * s) for i in range(groups)])
    shape = array(steps, k_block * v_sub, x_cells)
    keep, send = call(share_kernel, (shape, shape), place, *pieces, specs=[SMEM] + [VMEM] * steps)
    came = lax.ppermute(send, "gz", [(i, i ^ 1) for i in range(groups)])

    table = cas_square(y_cells)
    forward = call(forward_kernel, array(y_cells // 8, 2, 8, LANES), density.reshape(lines, y_cells), table, keep=True)
    buffers = [pltpu.VMEM(table.shape, BF16), pltpu.SemaphoreType.DMA]
    moved = lax.all_to_all(
        forward.reshape(pencils * groups, 8, LANES), ("pa", "gz"), split_axis=0, concat_axis=0, tiled=True
    )
    spectrum = call(
        spectrum_kernel,
        array(groups * 16, x_cells),
        moved.reshape(pencils, groups, 8, LANES),
        table,
        inside=(0,),
        specs=[VMEM, ANY],
        scratch_shapes=buffers,
    )

    turn = jnp.arange(steps, dtype=jnp.int32) * 2
    block = jnp.bitwise_xor(me, jnp.concatenate([turn, turn + 1]))
    k_index = (block[:, None] * k_block + jnp.arange(k_block, dtype=jnp.int32)[None, :]).reshape(-1)
    cos, sin = trig(k_index[:, None] * jnp.arange(z_cells, dtype=jnp.int32)[None, :], z_freqs)
    forth, inverse_z = call(
        lambda *refs: expand_kernel(*refs, v_sub=v_sub),
        (array(z_freqs * v_sub, groups * 16), array(groups * 16, z_freqs * v_sub)),
        (cos + sin).astype(BF16),
    )
    solved = call(
        solve_kernel,
        array(pencils, groups, 8, LANES),
        spectrum,
        forth,
        inverse_z,
        table,
        keep,
        came,
        specs=[VMEM, VMEM, VMEM, ANY, VMEM, VMEM],
        keep=True,
        scratch_shapes=buffers,
    )
    back = lax.all_to_all(
        solved.reshape(pencils * groups, 8, LANES), ("pa", "gz"), split_axis=0, concat_axis=0, tiled=True
    )
    scale = 1.0 / (x_cells * y_cells * z_freqs)
    out = call(
        lambda *refs: inverse_kernel(*refs, scale=scale),
        array(lines, y_cells, dtype=F32),
        back.reshape(y_cells // 8, 2, 8, LANES),
        table,
        inside=(0,),
        specs=[VMEM, ANY],
        scratch_shapes=buffers,
    )
    return out.reshape(z_slab, x_local, y_cells)


def solution(mesh):
    return jax.shard_map(
        local,
        mesh=mesh,
        in_specs=(P("gz", "pa", None), P("gz", "pa", None)),
        out_specs=P("gz", "pa", None),
        check_vma=False,
    )
```

profile of v0, /device:TPU:1, one launch (start us, length us, event | category | flops | bytes accessed | tf_op | source)
XLA Modules:
  0.0 112.3 jit_solution(9171716643002428569)
XLA Ops:
  0.0 0.0 copy-start.1
  0.0 0.5 fusion.19
  0.5 0.6 fusion.21
  1.1 0.6 add_convert_fusion
  1.8 0.0 copy-done.1
  1.8 1.5 %shard_map.28 = bf16[128,2,8,128]{3,2,1,0:T(8,128)(2,1)} custom-call(bf16[256,1024]{1,0:T(8,128)(2,1)S(1)} %bitcast.15, bf16[1024,1024]{1,0:T(8,128)(2,1)S(1)} %bitcast.8), custom_call_target="tpu_custom_call" | custom-call | tf_op jit(solution)/shard_map/pallas_call | solution.py:23
  3.3 15.6 %all-to-all-start = ((bf16[256,8,128]{2,1,0:T(8,128)(2,1)}), bf16[256,8,128]{2,1,0:T(8,128)(2,1)S(1)}, u32[]{:S(2)}, u32[]{:S(2)}) async-start(bf16[256,8,128]{2,1,0:T(8,128)(2,1)} %bitcast.2), calls=%async_computation | async-start | bytes 1048576 | tf_op jit(solution)/shard_map/all_to_all | solution.py:210
  19.0 0.0 copy-start
  19.0 1.6 %copy-done = f32[8,64,1024]{2,1,0:T(8,128)S(1)} copy-done((f32[8,64,1024]{2,1,0:T(8,128)S(1)}, f32[8,64,1024]{2,1,0:T(8,128)}, u32[]{:S(2)}) %copy-start) | copy-done | bytes 2097176
  20.6 0.4 shard_map.31
  21.0 1.6 %collective-permute-start = (bf16[64,1024]{1,0:T(8,128)(2,1)S(1)}, bf16[64,1024]{1,0:T(8,128)(2,1)S(1)}, u32[]{:S(2)}, u32[]{:S(2)}) collective-permute-start(bf16[64,1024]{1,0:T(8,128)(2,1)S(1)} %get-tuple-element.28), channel_id=1, source_target_pairs={{0,32},{16,48},{32,0},{48,16},{64,96},{80,112},{96,64},{112,80},{1... | collective-permute-start | bytes 393224 | tf_op jit(solution)/shard_map/ppermute | solution.py:202
  22.6 2.6 %collective-permute-start.1 = (bf16[64,1024]{1,0:T(8,128)(2,1)S(1)}, bf16[64,1024]{1,0:T(8,128)(2,1)S(1)}, u32[]{:S(2)}, u32[]{:S(2)}) collective-permute-start(bf16[64,1024]{1,0:T(8,128)(2,1)S(1)} %get-tuple-element.29), channel_id=1, source_target_pairs={{0,64},{16,80},{32,96},{48,112},{64,0},{80,16},{96,32},{112,48},{1... | collective-permute-start | bytes 393224 | tf_op jit(solution)/shard_map/ppermute | solution.py:202
  25.2 0.0 collective-permute-start.2
  25.2 5.6 %collective-permute-start.3 = (bf16[64,1024]{1,0:T(8,128)(2,1)S(1)}, bf16[64,1024]{1,0:T(8,128)(2,1)S(1)}, u32[]{:S(2)}, u32[]{:S(2)}) collective-permute-start(bf16[64,1024]{1,0:T(8,128)(2,1)S(1)} %get-tuple-element.31), channel_id=1, source_target_pairs={{0,128},{16,144},{32,160},{48,176},{64,192},{80,208},{96,224},{112... | collective-permute-start | bytes 393224 | tf_op jit(solution)/shard_map/ppermute | solution.py:202
  30.9 0.0 collective-permute-start.4
  30.9 5.5 %collective-permute-done.refs_1_ = bf16[64,1024]{1,0:T(8,128)(2,1)S(1)} collective-permute-done((bf16[64,1024]{1,0:T(8,128)(2,1)S(1)}, bf16[64,1024]{1,0:T(8,128)(2,1)S(1)}, u32[]{:S(2)}, u32[]{:S(2)}) %collective-permute-start) | collective-permute-done | bytes 131104 | tf_op jit(solution)/shard_map/ppermute | solution.py:202
  36.3 3.2 %collective-permute-start.5 = (bf16[64,1024]{1,0:T(8,128)(2,1)S(1)}, bf16[64,1024]{1,0:T(8,128)(2,1)S(1)}, u32[]{:S(2)}, u32[]{:S(2)}) collective-permute-start(bf16[64,1024]{1,0:T(8,128)(2,1)S(1)} %get-tuple-element.33), channel_id=1, source_target_pairs={{0,192},{16,208},{32,224},{48,240},{64,128},{80,144},{96,160},{112... | collective-permute-start | bytes 393224 | tf_op jit(solution)/shard_map/ppermute | solution.py:202
  39.5 0.0 collective-permute-done.1.refs_2_
  39.5 3.6 %collective-permute-start.6 = (bf16[64,1024]{1,0:T(8,128)(2,1)S(1)}, bf16[64,1024]{1,0:T(8,128)(2,1)S(1)}, u32[]{:S(2)}, u32[]{:S(2)}) collective-permute-start(bf16[64,1024]{1,0:T(8,128)(2,1)S(1)} %get-tuple-element.34), channel_id=1, source_target_pairs={{0,224},{16,240},{32,192},{48,208},{64,160},{80,176},{96,128},{112... | collective-permute-start | bytes 393224 | tf_op jit(solution)/shard_map/ppermute | solution.py:202
  43.2 6.8 %collective-permute-done.2.refs_3_ = bf16[64,1024]{1,0:T(8,128)(2,1)S(1)} collective-permute-done((bf16[64,1024]{1,0:T(8,128)(2,1)S(1)}, bf16[64,1024]{1,0:T(8,128)(2,1)S(1)}, u32[]{:S(2)}, u32[]{:S(2)}) %collective-permute-start.2) | collective-permute-done | bytes 131104 | tf_op jit(solution)/shard_map/ppermute | solution.py:202
  49.9 4.6 %collective-permute-done.3.refs_4_ = bf16[64,1024]{1,0:T(8,128)(2,1)S(1)} collective-permute-done((bf16[64,1024]{1,0:T(8,128)(2,1)S(1)}, bf16[64,1024]{1,0:T(8,128)(2,1)S(1)}, u32[]{:S(2)}, u32[]{:S(2)}) %collective-permute-start.3) | collective-permute-done | bytes 131104 | tf_op jit(solution)/shard_map/ppermute | solution.py:202
  54.5 2.9 %collective-permute-done.4.refs_5_ = bf16[64,1024]{1,0:T(8,128)(2,1)S(1)} collective-permute-done((bf16[64,1024]{1,0:T(8,128)(2,1)S(1)}, bf16[64,1024]{1,0:T(8,128)(2,1)S(1)}, u32[]{:S(2)}, u32[]{:S(2)}) %collective-permute-start.4) | collective-permute-done | bytes 131104 | tf_op jit(solution)/shard_map/ppermute | solution.py:202
  57.4 0.0 collective-permute-done.5.refs_6_
  57.4 0.0 collective-permute-done.6.refs_7_
  57.4 1.1 shard_map.32
  58.4 1.2 %collective-permute-start.7 = (bf16[8,32,1024]{2,1,0:T(8,128)(2,1)}, bf16[8,32,1024]{2,1,0:T(8,128)(2,1)}, u32[]{:S(2)}, u32[]{:S(2)}) collective-permute-start(bf16[8,32,1024]{2,1,0:T(8,128)(2,1)} %get-tuple-element.36), channel_id=1, source_target_pairs={{0,16},{16,0},{32,48},{48,32},{64,80},{80,64},{96,112},{112,96},{1... | collective-permute-start | bytes 1572872 | tf_op jit(solution)/shard_map/ppermute | solution.py:205
  59.7 0.1 fusion.24
  59.8 0.1 iota_add_fusion
  59.8 0.1 add.64
  59.9 0.3 add_convert_fusion.1.refs_0_
  60.3 0.4 shard_map.30
  60.7 0.0 copy-start.2
  60.7 0.7 copy-done.2
  61.4 0.0 all-to-all-done
  61.4 0.0 copy-start.3
  61.4 1.1 shard_map.29.spec_ref
  62.5 7.2 %collective-permute-done.7.came_ref = bf16[8,32,1024]{2,1,0:T(8,128)(2,1)} collective-permute-done((bf16[8,32,1024]{2,1,0:T(8,128)(2,1)}, bf16[8,32,1024]{2,1,0:T(8,128)(2,1)}, u32[]{:S(2)}, u32[]{:S(2)}) %collective-permute-start.7) | collective-permute-done | bytes 524320 | tf_op jit(solution)/shard_map/ppermute | solution.py:205
  69.7 0.0 copy-done.3
  69.7 2.7 %shard_map.33 = bf16[16,16,8,128]{3,2,1,0:T(8,128)(2,1)S(1)} custom-call(bf16[256,1024]{1,0:T(8,128)(2,1)S(1)} %shard_map.29.spec_ref, bf16[512,256]{1,0:T(8,128)(2,1)S(1)} %get-tuple-element.25.forth_ref, bf16[256,512]{1,0:T(8,128)(2,1)S(1)} %copy-done.3, bf16[1024,1024]{1,0:T(8,128)(2,1)S(1)} %bitcast.10, ...), custom_call_target="tpu_custom_call" | custom-call | tf_op jit(solution)/shard_map/pallas_call | solution.py:23
  72.4 37.7 %all_to_all.10 = bf16[256,8,128]{2,1,0:T(8,128)(2,1)S(1)} all-to-all(bf16[256,8,128]{2,1,0:T(8,128)(2,1)S(1)} %bitcast.12), channel_id=1, replica_groups=mesh['gz'=16,'pa'=16] {'pa','gz'}, dimensions={0} | all-to-all | bytes 1048576 | tf_op jit(solution)/shard_map/all_to_all | solution.py:245
  110.2 2.1 %shard_map.34 = f32[256,1024]{1,0:T(8,128)} custom-call(bf16[128,2,8,128]{3,2,1,0:T(8,128)(2,1)S(1)} %bitcast.13, bf16[1024,1024]{1,0:T(8,128)(2,1)S(1)} %bitcast.11), custom_call_target="tpu_custom_call" | custom-call | tf_op jit(solution)/shard_map/pallas_call | solution.py:23
  (2 shorter events, 0.0 us)
Async XLA Ops:
  0.0 1.8 %copy-start.1 = (bf16[4,64,1024]{2,1,0:T(8,128)(2,1)S(1)}, bf16[4,64,1024]{2,1,0:T(8,128)(2,1)}, u32[]{:S(2)}) copy-start(bf16[4,64,1024]{2,1,0:T(8,128)(2,1)} %param.2) | copy-start | bytes 1572868
  3.3 58.1 %all-to-all-start = ((bf16[256,8,128]{2,1,0:T(8,128)(2,1)}), bf16[256,8,128]{2,1,0:T(8,128)(2,1)S(1)}, u32[]{:S(2)}, u32[]{:S(2)}) async-start(bf16[256,8,128]{2,1,0:T(8,128)(2,1)} %bitcast.2), calls=%async_computation | async-start | bytes 1048576 | tf_op jit(solution)/shard_map/all_to_all | solution.py:210
  19.0 1.6 %copy-start = (f32[8,64,1024]{2,1,0:T(8,128)S(1)}, f32[8,64,1024]{2,1,0:T(8,128)}, u32[]{:S(2)}) copy-start(f32[8,64,1024]{2,1,0:T(8,128)} %green_ref.1) | copy-start | bytes 6291460
  21.0 15.3 %collective-permute-start = (bf16[64,1024]{1,0:T(8,128)(2,1)S(1)}, bf16[64,1024]{1,0:T(8,128)(2,1)S(1)}, u32[]{:S(2)}, u32[]{:S(2)}) collective-permute-start(bf16[64,1024]{1,0:T(8,128)(2,1)S(1)} %get-tuple-element.28), channel_id=1, source_target_pairs={{0,32},{16,48},{32,0},{48,16},{64,96},{80,112},{96,64},{112,80},{1... | collective-permute-start | bytes 393224 | tf_op jit(solution)/shard_map/ppermute | solution.py:202
  22.6 17.0 %collective-permute-start.1 = (bf16[64,1024]{1,0:T(8,128)(2,1)S(1)}, bf16[64,1024]{1,0:T(8,128)(2,1)S(1)}, u32[]{:S(2)}, u32[]{:S(2)}) collective-permute-start(bf16[64,1024]{1,0:T(8,128)(2,1)S(1)} %get-tuple-element.29), channel_id=1, source_target_pairs={{0,64},{16,80},{32,96},{48,112},{64,0},{80,16},{96,32},{112,48},{1... | collective-permute-start | bytes 393224 | tf_op jit(solution)/shard_map/ppermute | solution.py:202
  25.2 24.7 %collective-permute-start.2 = (bf16[64,1024]{1,0:T(8,128)(2,1)S(1)}, bf16[64,1024]{1,0:T(8,128)(2,1)S(1)}, u32[]{:S(2)}, u32[]{:S(2)}) collective-permute-start(bf16[64,1024]{1,0:T(8,128)(2,1)S(1)} %get-tuple-element.30), channel_id=1, source_target_pairs={{0,96},{16,112},{32,64},{48,80},{64,32},{80,48},{96,0},{112,16},{1... | collective-permute-start | bytes 393224 | tf_op jit(solution)/shard_map/ppermute | solution.py:202
  25.2 29.3 %collective-permute-start.3 = (bf16[64,1024]{1,0:T(8,128)(2,1)S(1)}, bf16[64,1024]{1,0:T(8,128)(2,1)S(1)}, u32[]{:S(2)}, u32[]{:S(2)}) collective-permute-start(bf16[64,1024]{1,0:T(8,128)(2,1)S(1)} %get-tuple-element.31), channel_id=1, source_target_pairs={{0,128},{16,144},{32,160},{48,176},{64,192},{80,208},{96,224},{112... | collective-permute-start | bytes 393224 | tf_op jit(solution)/shard_map/ppermute | solution.py:202
  30.9 26.5 %collective-permute-start.4 = (bf16[64,1024]{1,0:T(8,128)(2,1)S(1)}, bf16[64,1024]{1,0:T(8,128)(2,1)S(1)}, u32[]{:S(2)}, u32[]{:S(2)}) collective-permute-start(bf16[64,1024]{1,0:T(8,128)(2,1)S(1)} %get-tuple-element.32), channel_id=1, source_target_pairs={{0,160},{16,176},{32,128},{48,144},{64,224},{80,240},{96,192},{112... | collective-permute-start | bytes 393224 | tf_op jit(solution)/shard_map/ppermute | solution.py:202
  36.3 21.0 %collective-permute-start.5 = (bf16[64,1024]{1,0:T(8,128)(2,1)S(1)}, bf16[64,1024]{1,0:T(8,128)(2,1)S(1)}, u32[]{:S(2)}, u32[]{:S(2)}) collective-permute-start(bf16[64,1024]{1,0:T(8,128)(2,1)S(1)} %get-tuple-element.33), channel_id=1, source_target_pairs={{0,192},{16,208},{32,224},{48,240},{64,128},{80,144},{96,160},{112... | collective-permute-start | bytes 393224 | tf_op jit(solution)/shard_map/ppermute | solution.py:202
  39.5 17.8 %collective-permute-start.6 = (bf16[64,1024]{1,0:T(8,128)(2,1)S(1)}, bf16[64,1024]{1,0:T(8,128)(2,1)S(1)}, u32[]{:S(2)}, u32[]{:S(2)}) collective-permute-start(bf16[64,1024]{1,0:T(8,128)(2,1)S(1)} %get-tuple-element.34), channel_id=1, source_target_pairs={{0,224},{16,240},{32,192},{48,208},{64,160},{80,176},{96,128},{112... | collective-permute-start | bytes 393224 | tf_op jit(solution)/shard_map/ppermute | solution.py:202
  58.4 11.3 %collective-permute-start.7 = (bf16[8,32,1024]{2,1,0:T(8,128)(2,1)}, bf16[8,32,1024]{2,1,0:T(8,128)(2,1)}, u32[]{:S(2)}, u32[]{:S(2)}) collective-permute-start(bf16[8,32,1024]{2,1,0:T(8,128)(2,1)} %get-tuple-element.36), channel_id=1, source_target_pairs={{0,16},{16,0},{32,48},{48,32},{64,80},{80,64},{96,112},{112,96},{1... | collective-permute-start | bytes 1572872 | tf_op jit(solution)/shard_map/ppermute | solution.py:205
  60.7 0.7 copy-start.2
  61.4 8.3 %copy-start.3 = (bf16[256,512]{1,0:T(8,128)(2,1)S(1)}, bf16[256,512]{1,0:T(8,128)(2,1)}, u32[]{:S(2)}) copy-start(bf16[256,512]{1,0:T(8,128)(2,1)} %copy-done.2) | copy-start | bytes 786436
where the time goes:
time: 113 us; the launch traced here: 112 us
  blocking collectives  37.7 us (33%)
  starting transfers between devices  33.5 us (30%)
  waiting for transfers between devices  26.9 us (24%)
  Pallas kernels  9.35 us (8%)
  local copies, waits for them, and re-layouts  2.4 us (2%)
  other arithmetic  2.28 us (2%)
    all_to_all x1, blocking collectives, local(): lax.all_to_all(solved.reshape(pencils * groups, 8, LANES), ('pa', 'gz'),...  37.7 us
    ppermute x7, waiting for transfers between devices, local(): lax.ppermute(pieces[s], 'gz', [(i, i ^ 2 * s) for i in range(groups)])  19.7 us
    ppermute x7, starting transfers between devices, local(): lax.ppermute(pieces[s], 'gz', [(i, i ^ 2 * s) for i in range(groups)])  16.6 us
    all_to_all x1, starting transfers between devices, local(): lax.all_to_all(forward.reshape(pencils * groups, 8, LANES), ('pa', 'gz'),...  15.6 us
    pallas_call x7, Pallas kernels, call(): pl.pallas_call(kernel, out_shape=outs, in_specs=specs or [VMEM] * len(arg...  9.35 us
    ppermute x1, waiting for transfers between devices, local(): came = lax.ppermute(send, 'gz', [(i, i ^ 1) for i in range(groups)])  7.19 us
    unnamed x8, local copies, waits for them, and re-layouts  2.31 us
  transfers between devices with their start and end apart: 9, of which 5 were waited for; matrix products, arithmetic and copies ran while one was open for 1% of the time, Pallas kernels for 3%

commit v1 on v0

v1 whole, which is shorter than its diff:
```python
import math

import jax
import jax.numpy as jnp
from jax import lax
from jax.experimental import pallas as pl
from jax.experimental.pallas import tpu as pltpu
from jax.sharding import PartitionSpec as P


F32, BF16, I32 = jnp.float32, jnp.bfloat16, jnp.int32
LANES = 128
VMEM = pl.BlockSpec(memory_space=pltpu.VMEM)
SMEM = pl.BlockSpec(memory_space=pltpu.SMEM)
ANY = pl.BlockSpec(memory_space=pl.ANY)


def call(kernel, outs, *args, specs=None, keep=True, limit=24, **kwargs):
    specs = specs or [VMEM] * len(args)
    placed = []
    for a, s in zip(args, specs):
        placed.append(a if s is SMEM else pltpu.with_memory_space_constraint(a, pltpu.HBM if s is ANY else pltpu.VMEM))
    out_specs = jax.tree.map(lambda _: VMEM, outs)
    if keep:
        outs = jax.tree.map(lambda o: pltpu.VMEM(o.shape, o.dtype), outs)
    return pl.pallas_call(
        kernel,
        out_shape=outs,
        in_specs=specs,
        out_specs=out_specs,
        compiler_params=pltpu.CompilerParams(vmem_limit_bytes=limit * 2**20),
        **kwargs,
    )(*placed)


def array(*shape, dtype=BF16):
    return jax.ShapeDtypeStruct(shape, dtype)


def iota(shape, axis):
    return lax.broadcasted_iota(I32, shape, axis)


def trig(product, length):
    angle = lax.rem(product, jnp.full_like(product, length)).astype(F32) * (2.0 * math.pi / length)
    return jnp.cos(angle), jnp.sin(angle)


def cas_square(table_ref):
    length = table_ref.shape[0]
    coarse = length // 64
    k = iota((8, length), 1)
    cc, sc = trig(iota((8, length), 0) * k, length)
    cb, sb = trig(iota((8, length), 0) * 8 * k, length)
    high = [trig((iota((8, length), 0) + 8 * i) * 64 * k, length) for i in range(coarse // 8)]
    cbc = [cb[b : b + 1] * cc - sb[b : b + 1] * sc for b in range(8)]
    sbc = [sb[b : b + 1] * cc + cb[b : b + 1] * sc for b in range(8)]
    cbc, sbc = jnp.concatenate(cbc, axis=0), jnp.concatenate(sbc, axis=0)
    plus, minus = cbc + sbc, cbc - sbc
    for a in range(coarse):
        ca, sa = (x[a % 8 : a % 8 + 1] for x in high[a // 8])
        table_ref[64 * a : 64 * (a + 1)] = (ca * plus + sa * minus).astype(BF16)


def swap_halves(first, second, axis):
    half = first.shape[axis] // 2
    lower = iota(first.shape, axis) < half
    return (
        jnp.where(lower, first, pltpu.roll(second, half, axis)),
        jnp.where(lower, pltpu.roll(first, half, axis), second),
    )


def share(block, flip, keep_ref, send_ref, at):
    shape = keep_ref.shape[1:]
    block = block.reshape(block.shape[0] // 16, 2, 8, block.shape[1])
    low, high = swap_halves(block[:, 0], block[:, 1], 1)
    keep_ref[at] = jnp.where(flip == 0, low, high).reshape(shape).astype(BF16)
    send_ref[at] = jnp.where(flip == 0, high, low).reshape(shape).astype(BF16)


def split_kernel(me_ref, green_ref, keep_ref, send_ref, *refs, near, far, steps):
    *far_refs, buffer, sems = refs
    copies = []
    for i, s in enumerate(near + far):
        at = pl.multiple_of(along_z(me_ref[0] // 2, s, steps) * 8, 8)
        copies.append(pltpu.make_async_copy(green_ref.at[:, pl.ds(at, 8), :], buffer.at[i], sems.at[i]))
        copies[-1].start()
    for i in range(len(near + far)):
        copies[i].wait()
        block = buffer[i]
        block = block.reshape(block.shape[0] * block.shape[1], block.shape[2])
        if i < len(near):
            share(block, me_ref[0] % 2, keep_ref, send_ref, i)
        else:
            far_refs[i - len(near)][...] = block.astype(BF16)


def share_kernel(me_ref, *refs):
    *in_refs, keep_ref, send_ref = refs
    for i, in_ref in enumerate(in_refs):
        share(in_ref[...].astype(F32), me_ref[0] % 2, keep_ref, send_ref, i)


def join_kernel(keep_ref, came_ref, *out_refs):
    rows = keep_ref.shape[1]
    for i, out_ref in enumerate(out_refs):
        out_ref[:rows] = keep_ref[i + 1]
        out_ref[rows:] = came_ref[i + 1]


def expand_kernel(me_ref, forth_ref, back_ref, *, order, groups, v_sub, k_block, z_slab):
    rows, cols = forth_ref.shape
    half, steps = cols // 2, groups // 2
    freqs, cells = groups * k_block, groups * z_slab
    r = iota((freqs, cells), 0)
    step, turn = jnp.zeros_like(r), jnp.zeros_like(r)
    for i, (s, sy) in enumerate(order):
        step = jnp.where(r // k_block == i, s, step)
        turn = jnp.where(r // k_block == i, sy, turn)
    from_z = along_z(me_ref[0] // 2, step, steps, sign=-1)
    from_y = jnp.bitwise_xor(me_ref[0] % 2, turn)
    cos, sin = trig(((from_z * 2 + from_y) * k_block + r % k_block) * iota((freqs, cells), 1), freqs)
    small = (cos + sin).astype(BF16)

    def z_of(c):
        return c % half // 8 * z_slab + c // v_sub % 2 * 2 + c // half

    def ones(mask):
        return jnp.where(mask, 1.0, 0.0).astype(BF16)

    spread = ones(iota((rows, freqs), 0) // v_sub == iota((rows, freqs), 1))
    pick = ones(iota((cells, cols), 0) == z_of(iota((cells, cols), 1)))
    full = jnp.dot(jnp.dot(spread, small, preferred_element_type=F32).astype(BF16), pick, preferred_element_type=F32)
    same = iota((rows, cols), 0) % v_sub == iota((rows, cols), 1) % v_sub
    forth_ref[...] = jnp.where(same, full, 0.0).astype(BF16)
    pick = ones(z_of(iota((cols, cells), 0)) == iota((cols, cells), 1))
    spread = ones(iota((freqs, rows), 1) // v_sub == iota((freqs, rows), 0))
    part = lax.dot_general(pick, small, (((1,), (1,)), ((), ())), preferred_element_type=F32).astype(BF16)
    full = jnp.dot(part, spread, preferred_element_type=F32)
    same = iota((cols, rows), 0) % v_sub == iota((cols, rows), 1) % v_sub
    back_ref[...] = jnp.where(same, full, 0.0).astype(BF16)


def forward_kernel(density_ref, out_ref, table_ref):
    cas_square(table_ref)
    spec = lax.dot_general(table_ref[...], density_ref[...], (((1,), (1,)), ((), ())), preferred_element_type=F32)
    tiles = spec.shape[0] // 8
    left = spec[:, :LANES].reshape(tiles, 8, LANES)
    right = spec[:, LANES:].reshape(tiles, 8, LANES)
    even, odd = swap_halves(left, right, 1)
    out_ref[:, 0] = even.astype(BF16)
    out_ref[:, 1] = odd.astype(BF16)


def spectrum_kernel(moved_ref, table_ref, out_ref):
    pencils, groups = moved_ref.shape[:2]
    rows = groups * 8
    low, high = [], []
    for q in range(pencils // 2):
        left = moved_ref[2 * q].reshape(rows, LANES).astype(F32)
        right = moved_ref[2 * q + 1].reshape(rows, LANES).astype(F32)
        a, b = swap_halves(left, right, 1)
        low.append(a.astype(BF16))
        high.append(b.astype(BF16))
    data = jnp.concatenate([jnp.concatenate(low, axis=1), jnp.concatenate(high, axis=1)], axis=0)
    out_ref[...] = jnp.dot(data, table_ref[...], preferred_element_type=F32).astype(BF16)


def solve_kernel(spec_ref, forth_ref, back_ref, table_ref, *refs):
    *near_refs, keep_near_ref, keep_far_ref, came_near_ref, came_far_ref, out_ref = refs
    zspec = jnp.dot(forth_ref[...], spec_ref[...], preferred_element_type=F32)
    blocks = [ref[...] for ref in near_refs]
    for near_ref, far_ref in ((keep_near_ref, keep_far_ref), (came_near_ref, came_far_ref)):
        blocks.append(near_ref[0])
        blocks.extend(far_ref[i] for i in range(far_ref.shape[0]))
    parts, at = [], 0
    for block in blocks:
        parts.append((zspec[at : at + block.shape[0]] * block.astype(F32)).astype(BF16))
        at += block.shape[0]
    weighted = jnp.concatenate(parts, axis=0)
    total = jnp.dot(back_ref[...], weighted, preferred_element_type=F32).astype(BF16)
    values = jnp.dot(total, table_ref[...], preferred_element_type=F32)
    half = values.shape[0] // 2
    shape = out_ref.shape[1:]
    for q in range(out_ref.shape[0] // 2):
        at = slice(q * LANES, (q + 1) * LANES)
        a, b = swap_halves(values[:half, at], values[half:, at], 1)
        out_ref[2 * q] = a.astype(BF16).reshape(shape)
        out_ref[2 * q + 1] = b.astype(BF16).reshape(shape)


def inverse_kernel(came_ref, table_ref, out_ref, *, scale):
    left, right = swap_halves(came_ref[:, 0].astype(F32), came_ref[:, 1].astype(F32), 1)
    rows = left.shape[0] * 8
    data = jnp.concatenate([left.reshape(rows, LANES), right.reshape(rows, LANES)], axis=1).astype(BF16)
    out = lax.dot_general(data, table_ref[...], (((0,), (0,)), ((), ())), preferred_element_type=F32)
    out_ref[...] = out * scale


def along_z(z, s, steps, sign=1):
    return (z + sign * s) & (steps - 1)


def local(density, green):
    z_slab, x_local, y_cells = density.shape
    k_block, y_local, x_cells = green.shape
    groups = lax.axis_size("gz")
    pencils = lax.axis_size("pa")
    v_sub = y_local // groups
    z_freqs = k_block * groups
    lines = z_slab * x_local
    steps = groups // 2
    place = lax.axis_index("gz").astype(I32).reshape(1)

    near, far = (0, 1, steps - 1, 2, steps - 2), tuple(range(3, steps - 2))
    order = [(s, sy) for s in near[1:] for sy in (0, 1)] + [(s, sy) for sy in (0, 1) for s in (0, *far)]

    def shift_z(piece, s):
        pairs = [(i, along_z(i // 2, s, steps) * 2 + i % 2) for i in range(groups)]
        return lax.ppermute(piece, "gz", pairs)

    def swap_y(piece):
        return lax.ppermute(piece, "gz", [(i, i ^ 1) for i in range(groups)])

    rows = k_block * v_sub
    shared = array(len(near), rows, x_cells)
    keep_near, send_near, *outward = call(
        lambda *refs: split_kernel(*refs, near=near, far=far, steps=steps),
        (shared, shared) + (array(2 * rows, x_cells),) * len(far),
        place,
        green,
        specs=[SMEM, ANY],
        scratch_shapes=[pltpu.VMEM((steps, k_block, 2 * v_sub, x_cells), F32), pltpu.SemaphoreType.DMA((steps,))],
    )
    came_near = swap_y(send_near)
    inward = [shift_z(piece, s) for piece, s in zip(outward, far)]
    shared = array(len(far), rows, x_cells)
    keep_far, send_far = call(share_kernel, (shared, shared), place, *inward, specs=[SMEM] + [VMEM] * len(far))
    came_far = swap_y(send_far)
    pieces = call(join_kernel, (array(2 * rows, x_cells),) * (len(near) - 1), keep_near, came_near)
    pieces = [shift_z(piece, s) for piece, s in zip(pieces, near[1:])]

    forward, table = call(
        forward_kernel, (array(y_cells // 8, 2, 8, LANES), array(y_cells, y_cells)), density.reshape(lines, y_cells)
    )
    moved = lax.all_to_all(
        forward.reshape(pencils * groups, 8, LANES), ("pa", "gz"), split_axis=0, concat_axis=0, tiled=True
    )
    spectrum = call(spectrum_kernel, array(groups * 16, x_cells), moved.reshape(pencils, groups, 8, LANES), table)
    forth, inverse_z = call(
        lambda *refs: expand_kernel(*refs, order=order, groups=groups, v_sub=v_sub, k_block=k_block, z_slab=z_slab),
        (array(z_freqs * v_sub, groups * 16), array(groups * 16, z_freqs * v_sub)),
        place,
        specs=[SMEM],
    )
    solved = call(
        solve_kernel,
        array(pencils, groups, 8, LANES),
        spectrum,
        forth,
        inverse_z,
        table,
        *pieces,
        keep_near,
        keep_far,
        came_near,
        came_far,
    )
    back = lax.all_to_all(
        solved.reshape(pencils * groups, 8, LANES), ("pa", "gz"), split_axis=0, concat_axis=0, tiled=True
    )
    scale = 1.0 / (x_cells * y_cells * z_freqs)
    out = call(
        lambda *refs: inverse_kernel(*refs, scale=scale),
        array(lines, y_cells, dtype=F32),
        back.reshape(y_cells // 8, 2, 8, LANES),
        table,
        keep=False,
    )
    return out.reshape(z_slab, x_local, y_cells)


def solution(mesh):
    return jax.shard_map(
        local,
        mesh=mesh,
        in_specs=(P("gz", "pa", None), P("gz", "pa", None)),
        out_specs=P("gz", "pa", None),
        check_vma=False,
    )
```

time: 113 us -> 101 us (0.89)
  waiting for transfers between devices: 26.9 us -> 21.2 us
  blocking collectives: 37.7 us -> 32.9 us
  other arithmetic: 2.28 us -> 0 us
  Pallas kernels: 9.35 us -> 11.3 us
    ppermute x8 -> x9, waiting for transfers between devices: 26.9 us -> 21.2 us  [the longest x7 21.1 us: shift_z(): return lax.ppermute(piece, 'gz', pairs)]
    all_to_all x1, blocking collectives: 37.7 us -> 32.9 us  [local(): lax.all_to_all(solved.reshape(pencils * groups, 8, LANES), ('pa', 'gz'),...]
    pallas_call x7 -> x8, Pallas kernels: 9.35 us -> 11.3 us  [call(): pl.pallas_call(kernel, out_shape=outs, in_specs=specs, out_specs=out_spec...]
    unnamed x8 -> x10, local copies, waits for them, and re-layouts: 2.31 us -> 1.75 us
    ppermute x8 -> x9, starting transfers between devices: 17.9 us -> 18.3 us  [the longest x7 16.8 us: shift_z(): return lax.ppermute(piece, 'gz', pairs)]
  transfers between devices with their start and end apart: 9 -> 10, of which waited for: 5 -> 4; matrix products, arithmetic and copies ran while one was open for 1% -> 0% of each run, Pallas kernels for 3% -> 5%
where the time goes in v1:
time: 101 us
  starting transfers between devices  33.9 us (34%)
  blocking collectives  32.9 us (33%)
  waiting for transfers between devices  21.2 us (21%)
  Pallas kernels  11.3 us (11%)
  local copies, waits for them, and re-layouts  1.75 us (2%)
    all_to_all x1, blocking collectives, local(): lax.all_to_all(solved.reshape(pencils * groups, 8, LANES), ('pa', 'gz'),...  32.9 us
    ppermute x7, waiting for transfers between devices, shift_z(): return lax.ppermute(piece, 'gz', pairs)  21.1 us
    ppermute x7, starting transfers between devices, shift_z(): return lax.ppermute(piece, 'gz', pairs)  16.8 us
    all_to_all x1, starting transfers between devices, local(): lax.all_to_all(forward.reshape(pencils * groups, 8, LANES), ('pa', 'gz'),...  15.6 us
    pallas_call x8, Pallas kernels, call(): pl.pallas_call(kernel, out_shape=outs, in_specs=specs, out_specs=out_spec...  11.3 us
  transfers between devices with their start and end apart: 10, of which 4 were waited for; matrix products, arithmetic and copies ran while one was open for 0% of the time, Pallas kernels for 5%

profile of v1, /device:TPU:1, one launch (start us, length us, event | category | flops | bytes accessed | tf_op | source)
XLA Modules:
  0.0 101.1 jit_solution(5206655464980740454)
XLA Ops:
  0.0 0.0 copy-start
  0.0 1.0 %copy-done = bf16[4,64,1024]{2,1,0:T(8,128)(2,1)S(1)} copy-done((bf16[4,64,1024]{2,1,0:T(8,128)(2,1)S(1)}, bf16[4,64,1024]{2,1,0:T(8,128)(2,1)}, u32[]{:S(2)}) %copy-start) | copy-done | bytes 524312
  1.0 2.3 %shard_map.28 = (bf16[128,2,8,128]{3,2,1,0:T(8,128)(2,1)}, bf16[1024,1024]{1,0:T(8,128)(2,1)S(1)}) custom-call(bf16[256,1024]{1,0:T(8,128)(2,1)S(1)} %bitcast.10), custom_call_target="tpu_custom_call" | custom-call | tf_op jit(solution)/shard_map/pallas_call | solution.py:26
  3.3 15.6 %all-to-all-start = ((bf16[256,8,128]{2,1,0:T(8,128)(2,1)}), bf16[256,8,128]{2,1,0:T(8,128)(2,1)S(1)}, u32[]{:S(2)}, u32[]{:S(2)}) async-start(bf16[256,8,128]{2,1,0:T(8,128)(2,1)} %bitcast.1), calls=%async_computation | async-start | bytes 1048576 | tf_op jit(solution)/shard_map/all_to_all | solution.py:247
  19.0 1.6 %shard_map.31 = (bf16[5,32,1024]{2,1,0:T(8,128)(2,1)S(1)}, bf16[5,32,1024]{2,1,0:T(8,128)(2,1)S(1)}, bf16[64,1024]{1,0:T(8,128)(2,1)S(1)}, bf16[64,1024]{1,0:T(8,128)(2,1)S(1)}, bf16[64,1024]{1,0:T(8,128)(2,1)S(1)}) custom-call(s32[1]{0:T(128)} %bitcast.3.refs_0_.me_ref, f32[8,64,1024]{2,1,0:T(8,128)} %refs_1_.1), custom_call_target="tpu_custom_call" | custom-call | tf_op jit(solution)/shard_map/pallas_call | solution.py:26
  20.6 1.4 %collective-permute-start = (bf16[5,32,1024]{2,1,0:T(8,128)(2,1)S(1)}, bf16[5,32,1024]{2,1,0:T(8,128)(2,1)S(1)}, u32[]{:S(2)}, u32[]{:S(2)}) collective-permute-start(bf16[5,32,1024]{2,1,0:T(8,128)(2,1)S(1)} %get-tuple-element.25), channel_id=1, source_target_pairs={{0,16},{16,0},{32,48},{48,32},{64,80},{80,64},{96,112},{112,96},{1... | collective-permute-start | bytes 983048 | tf_op jit(solution)/shard_map/ppermute | solution.py:224
  22.0 3.7 %collective-permute-start.5 = (bf16[64,1024]{1,0:T(8,128)(2,1)S(1)}, bf16[64,1024]{1,0:T(8,128)(2,1)S(1)}, u32[]{:S(2)}, u32[]{:S(2)}) collective-permute-start(bf16[64,1024]{1,0:T(8,128)(2,1)S(1)} %get-tuple-element.30), channel_id=1, source_target_pairs={{0,96},{16,112},{32,128},{48,144},{64,160},{80,176},{96,192},{112,... | collective-permute-start | bytes 393224 | tf_op jit(solution)/shard_map/ppermute | solution.py:221
  25.8 3.5 %collective-permute-start.6 = (bf16[64,1024]{1,0:T(8,128)(2,1)S(1)}, bf16[64,1024]{1,0:T(8,128)(2,1)S(1)}, u32[]{:S(2)}, u32[]{:S(2)}) collective-permute-start(bf16[64,1024]{1,0:T(8,128)(2,1)S(1)} %get-tuple-element.31), channel_id=1, source_target_pairs={{0,128},{16,144},{32,160},{48,176},{64,192},{80,208},{96,224},{112... | collective-permute-start | bytes 393224 | tf_op jit(solution)/shard_map/ppermute | solution.py:221
  29.2 3.4 %collective-permute-start.7 = (bf16[64,1024]{1,0:T(8,128)(2,1)S(1)}, bf16[64,1024]{1,0:T(8,128)(2,1)S(1)}, u32[]{:S(2)}, u32[]{:S(2)}) collective-permute-start(bf16[64,1024]{1,0:T(8,128)(2,1)S(1)} %get-tuple-element.32), channel_id=1, source_target_pairs={{0,160},{16,176},{32,192},{48,208},{64,224},{80,240},{96,0},{112,1... | collective-permute-start | bytes 393224 | tf_op jit(solution)/shard_map/ppermute | solution.py:221
  32.6 11.4 %collective-permute-done.5.refs_0_ = bf16[64,1024]{1,0:T(8,128)(2,1)S(1)} collective-permute-done((bf16[64,1024]{1,0:T(8,128)(2,1)S(1)}, bf16[64,1024]{1,0:T(8,128)(2,1)S(1)}, u32[]{:S(2)}, u32[]{:S(2)}) %collective-permute-start.5) | collective-permute-done | bytes 131104 | tf_op jit(solution)/shard_map/ppermute | solution.py:221
  44.0 5.5 %collective-permute-done.6.refs_1_ = bf16[64,1024]{1,0:T(8,128)(2,1)S(1)} collective-permute-done((bf16[64,1024]{1,0:T(8,128)(2,1)S(1)}, bf16[64,1024]{1,0:T(8,128)(2,1)S(1)}, u32[]{:S(2)}, u32[]{:S(2)}) %collective-permute-start.6) | collective-permute-done | bytes 131104 | tf_op jit(solution)/shard_map/ppermute | solution.py:221
  49.6 0.0 collective-permute-done.7.refs_2_
  49.6 0.8 shard_map.33
  50.4 0.0 copy-start.3
  50.4 0.0 collective-permute-start.8
  50.4 0.0 collective-permute-done.came_ref.refs_6_
  50.4 0.9 shard_map.32
  51.2 0.8 collective-permute-start.1
  52.1 1.8 %collective-permute-start.2 = (bf16[64,1024]{1,0:T(8,128)(2,1)}, bf16[64,1024]{1,0:T(8,128)(2,1)}, u32[]{:S(2)}, u32[]{:S(2)}) collective-permute-start(bf16[64,1024]{1,0:T(8,128)(2,1)} %get-tuple-element.27), channel_id=1, source_target_pairs={{0,224},{16,240},{32,0},{48,16},{64,32},{80,48},{96,64},{112,80},{... | collective-permute-start | bytes 393224 | tf_op jit(solution)/shard_map/ppermute | solution.py:221
  53.9 0.4 collective-permute-start.3
  54.3 3.1 %collective-permute-start.4 = (bf16[64,1024]{1,0:T(8,128)(2,1)}, bf16[64,1024]{1,0:T(8,128)(2,1)}, u32[]{:S(2)}, u32[]{:S(2)}) collective-permute-start(bf16[64,1024]{1,0:T(8,128)(2,1)} %get-tuple-element.29), channel_id=1, source_target_pairs={{0,192},{16,208},{32,224},{48,240},{64,0},{80,16},{96,32},{112,48}... | collective-permute-start | bytes 393224 | tf_op jit(solution)/shard_map/ppermute | solution.py:221
  57.5 0.0 copy-done.3
  57.5 0.7 shard_map.30
  58.2 0.0 copy-start.1
  58.2 0.7 copy-done.1
  58.9 0.0 all-to-all-done
  58.9 0.0 copy-start.2
  58.9 0.0 copy-start.4
  58.9 0.8 shard_map.29.spec_ref
  59.7 0.0 collective-permute-done.8.refs_7_
  59.7 0.0 collective-permute-done.1.refs_0_
  59.7 0.0 collective-permute-done.2.refs_1_
  59.7 1.5 %collective-permute-done.3.refs_2_ = bf16[64,1024]{1,0:T(8,128)(2,1)} collective-permute-done((bf16[64,1024]{1,0:T(8,128)(2,1)}, bf16[64,1024]{1,0:T(8,128)(2,1)}, u32[]{:S(2)}, u32[]{:S(2)}) %collective-permute-start.3) | collective-permute-done | bytes 131104 | tf_op jit(solution)/shard_map/ppermute | solution.py:221
  61.2 2.7 %collective-permute-done.4.refs_3_ = bf16[64,1024]{1,0:T(8,128)(2,1)} collective-permute-done((bf16[64,1024]{1,0:T(8,128)(2,1)}, bf16[64,1024]{1,0:T(8,128)(2,1)}, u32[]{:S(2)}, u32[]{:S(2)}) %collective-permute-start.4) | collective-permute-done | bytes 131104 | tf_op jit(solution)/shard_map/ppermute | solution.py:221
  63.9 0.0 copy-done.2
  63.9 0.0 copy-done.4
  63.9 2.5 %shard_map.34 = bf16[16,16,8,128]{3,2,1,0:T(8,128)(2,1)S(1)} custom-call(bf16[256,1024]{1,0:T(8,128)(2,1)S(1)} %shard_map.29.spec_ref, bf16[512,256]{1,0:T(8,128)(2,1)S(1)} %get-tuple-element.22.forth_ref, bf16[256,512]{1,0:T(8,128)(2,1)S(1)} %copy-done.2, bf16[1024,1024]{1,0:T(8,128)(2,1)S(1)} %get-tuple-element.21.table_ref.refs_1_, ...), custom_call_target="tpu_custom_call" | custom-call | tf_op jit(solution)/shard_map/pallas_call | solution.py:26
  66.4 32.9 %all_to_all.10 = bf16[256,8,128]{2,1,0:T(8,128)(2,1)S(1)} all-to-all(bf16[256,8,128]{2,1,0:T(8,128)(2,1)S(1)} %bitcast.7), channel_id=1, replica_groups=mesh['gz'=16,'pa'=16] {'pa','gz'}, dimensions={0} | all-to-all | bytes 1048576 | tf_op jit(solution)/shard_map/all_to_all | solution.py:270
  99.4 1.7 %shard_map.35 = f32[256,1024]{1,0:T(8,128)} custom-call(bf16[128,2,8,128]{3,2,1,0:T(8,128)(2,1)S(1)} %bitcast.8, bf16[1024,1024]{1,0:T(8,128)(2,1)S(1)} %get-tuple-element.21.table_ref.refs_1_), custom_call_target="tpu_custom_call" | custom-call | tf_op jit(solution)/shard_map/pallas_call | solution.py:26
Async XLA Ops:
  0.0 1.0 %copy-start = (bf16[4,64,1024]{2,1,0:T(8,128)(2,1)S(1)}, bf16[4,64,1024]{2,1,0:T(8,128)(2,1)}, u32[]{:S(2)}) copy-start(bf16[4,64,1024]{2,1,0:T(8,128)(2,1)} %param.2) | copy-start | bytes 1572868
  3.3 55.6 %all-to-all-start = ((bf16[256,8,128]{2,1,0:T(8,128)(2,1)}), bf16[256,8,128]{2,1,0:T(8,128)(2,1)S(1)}, u32[]{:S(2)}, u32[]{:S(2)}) async-start(bf16[256,8,128]{2,1,0:T(8,128)(2,1)} %bitcast.1), calls=%async_computation | async-start | bytes 1048576 | tf_op jit(solution)/shard_map/all_to_all | solution.py:247
  20.6 29.8 %collective-permute-start = (bf16[5,32,1024]{2,1,0:T(8,128)(2,1)S(1)}, bf16[5,32,1024]{2,1,0:T(8,128)(2,1)S(1)}, u32[]{:S(2)}, u32[]{:S(2)}) collective-permute-start(bf16[5,32,1024]{2,1,0:T(8,128)(2,1)S(1)} %get-tuple-element.25), channel_id=1, source_target_pairs={{0,16},{16,0},{32,48},{48,32},{64,80},{80,64},{96,112},{112,96},{1... | collective-permute-start | bytes 983048 | tf_op jit(solution)/shard_map/ppermute | solution.py:224
  22.0 22.0 %collective-permute-start.5 = (bf16[64,1024]{1,0:T(8,128)(2,1)S(1)}, bf16[64,1024]{1,0:T(8,128)(2,1)S(1)}, u32[]{:S(2)}, u32[]{:S(2)}) collective-permute-start(bf16[64,1024]{1,0:T(8,128)(2,1)S(1)} %get-tuple-element.30), channel_id=1, source_target_pairs={{0,96},{16,112},{32,128},{48,144},{64,160},{80,176},{96,192},{112,... | collective-permute-start | bytes 393224 | tf_op jit(solution)/shard_map/ppermute | solution.py:221
  25.8 23.8 %collective-permute-start.6 = (bf16[64,1024]{1,0:T(8,128)(2,1)S(1)}, bf16[64,1024]{1,0:T(8,128)(2,1)S(1)}, u32[]{:S(2)}, u32[]{:S(2)}) collective-permute-start(bf16[64,1024]{1,0:T(8,128)(2,1)S(1)} %get-tuple-element.31), channel_id=1, source_target_pairs={{0,128},{16,144},{32,160},{48,176},{64,192},{80,208},{96,224},{112... | collective-permute-start | bytes 393224 | tf_op jit(solution)/shard_map/ppermute | solution.py:221
  29.2 20.3 %collective-permute-start.7 = (bf16[64,1024]{1,0:T(8,128)(2,1)S(1)}, bf16[64,1024]{1,0:T(8,128)(2,1)S(1)}, u32[]{:S(2)}, u32[]{:S(2)}) collective-permute-start(bf16[64,1024]{1,0:T(8,128)(2,1)S(1)} %get-tuple-element.32), channel_id=1, source_target_pairs={{0,160},{16,176},{32,192},{48,208},{64,224},{80,240},{96,0},{112,1... | collective-permute-start | bytes 393224 | tf_op jit(solution)/shard_map/ppermute | solution.py:221
  50.4 7.1 %copy-start.3 = (bf16[3,32,1024]{2,1,0:T(8,128)(2,1)}, bf16[3,32,1024]{2,1,0:T(8,128)(2,1)S(1)}, u32[]{:S(2)}) copy-start(bf16[3,32,1024]{2,1,0:T(8,128)(2,1)S(1)} %get-tuple-element.33.refs_5_) | copy-start | bytes 589828
  50.4 9.3 %collective-permute-start.8 = (bf16[3,32,1024]{2,1,0:T(8,128)(2,1)}, bf16[3,32,1024]{2,1,0:T(8,128)(2,1)}, u32[]{:S(2)}, u32[]{:S(2)}) collective-permute-start(bf16[3,32,1024]{2,1,0:T(8,128)(2,1)} %get-tuple-element.34), channel_id=1, source_target_pairs={{0,16},{16,0},{32,48},{48,32},{64,80},{80,64},{96,112},{112,96},{1... | collective-permute-start | bytes 589832 | tf_op jit(solution)/shard_map/ppermute | solution.py:224
  51.2 8.5 %collective-permute-start.1 = (bf16[64,1024]{1,0:T(8,128)(2,1)}, bf16[64,1024]{1,0:T(8,128)(2,1)}, u32[]{:S(2)}, u32[]{:S(2)}) collective-permute-start(bf16[64,1024]{1,0:T(8,128)(2,1)} %get-tuple-element.26), channel_id=1, source_target_pairs={{0,32},{16,48},{32,64},{48,80},{64,96},{80,112},{96,128},{112,144}... | collective-permute-start | bytes 393224 | tf_op jit(solution)/shard_map/ppermute | solution.py:221
  52.1 7.6 %collective-permute-start.2 = (bf16[64,1024]{1,0:T(8,128)(2,1)}, bf16[64,1024]{1,0:T(8,128)(2,1)}, u32[]{:S(2)}, u32[]{:S(2)}) collective-permute-start(bf16[64,1024]{1,0:T(8,128)(2,1)} %get-tuple-element.27), channel_id=1, source_target_pairs={{0,224},{16,240},{32,0},{48,16},{64,32},{80,48},{96,64},{112,80},{... | collective-permute-start | bytes 393224 | tf_op jit(solution)/shard_map/ppermute | solution.py:221
  53.9 7.3 %collective-permute-start.3 = (bf16[64,1024]{1,0:T(8,128)(2,1)}, bf16[64,1024]{1,0:T(8,128)(2,1)}, u32[]{:S(2)}, u32[]{:S(2)}) collective-permute-start(bf16[64,1024]{1,0:T(8,128)(2,1)} %get-tuple-element.28), channel_id=1, source_target_pairs={{0,64},{16,80},{32,96},{48,112},{64,128},{80,144},{96,160},{112,17... | collective-permute-start | bytes 393224 | tf_op jit(solution)/shard_map/ppermute | solution.py:221
  54.3 9.5 %collective-permute-start.4 = (bf16[64,1024]{1,0:T(8,128)(2,1)}, bf16[64,1024]{1,0:T(8,128)(2,1)}, u32[]{:S(2)}, u32[]{:S(2)}) collective-permute-start(bf16[64,1024]{1,0:T(8,128)(2,1)} %get-tuple-element.29), channel_id=1, source_target_pairs={{0,192},{16,208},{32,224},{48,240},{64,0},{80,16},{96,32},{112,48}... | collective-permute-start | bytes 393224 | tf_op jit(solution)/shard_map/ppermute | solution.py:221
  58.2 0.7 copy-start.1
  58.9 5.0 %copy-start.2 = (bf16[256,512]{1,0:T(8,128)(2,1)S(1)}, bf16[256,512]{1,0:T(8,128)(2,1)}, u32[]{:S(2)}) copy-start(bf16[256,512]{1,0:T(8,128)(2,1)} %copy-done.1) | copy-start | bytes 786436
  58.9 5.0 %copy-start.4 = (bf16[3,32,1024]{2,1,0:T(8,128)(2,1)S(1)}, bf16[3,32,1024]{2,1,0:T(8,128)(2,1)}, u32[]{:S(2)}) copy-start(bf16[3,32,1024]{2,1,0:T(8,128)(2,1)} %copy-done.3) | copy-start | bytes 589828

commit v2 on v1

--- a/solution.py
+++ b/solution.py
@@ -15,22 +15,26 @@
 ANY = pl.BlockSpec(memory_space=pl.ANY)
 
 
-def call(kernel, outs, *args, specs=None, keep=True, limit=24, **kwargs):
+def call(kernel, outs, *args, specs=None, results=None, limit=24, **kwargs):
     specs = specs or [VMEM] * len(args)
     placed = []
     for a, s in zip(args, specs):
         placed.append(a if s is SMEM else pltpu.with_memory_space_constraint(a, pltpu.HBM if s is ANY else pltpu.VMEM))
-    out_specs = jax.tree.map(lambda _: VMEM, outs)
-    if keep:
-        outs = jax.tree.map(lambda o: pltpu.VMEM(o.shape, o.dtype), outs)
+    results = results or jax.tree.map(lambda _: VMEM, outs)
     return pl.pallas_call(
         kernel,
         out_shape=outs,
         in_specs=specs,
-        out_specs=out_specs,
+        out_specs=results,
         compiler_params=pltpu.CompilerParams(vmem_limit_bytes=limit * 2**20),
         **kwargs,
     )(*placed)
+
+
+def send(buffer, out_ref, sem):
+    copy = pltpu.make_async_copy(buffer, out_ref, sem)
+    copy.start()
+    return copy
 
 
 def array(*shape, dtype=BF16):
@@ -80,20 +84,25 @@
 
 
 def split_kernel(me_ref, green_ref, keep_ref, send_ref, *refs, near, far, steps):
-    *far_refs, buffer, sems = refs
-    copies = []
-    for i, s in enumerate(near + far):
+    *far_refs, buffer, near_buffer, far_buffer, sems, out_sems = refs
+    copies, sent = [], []
+    for i, s in enumerate(far + near):
         at = pl.multiple_of(along_z(me_ref[0] // 2, s, steps) * 8, 8)
         copies.append(pltpu.make_async_copy(green_ref.at[:, pl.ds(at, 8), :], buffer.at[i], sems.at[i]))
         copies[-1].start()
-    for i in range(len(near + far)):
+    for i in range(len(far + near)):
         copies[i].wait()
         block = buffer[i]
         block = block.reshape(block.shape[0] * block.shape[1], block.shape[2])
-        if i < len(near):
-            share(block, me_ref[0] % 2, keep_ref, send_ref, i)
+        n = i - len(far)
+        if n < 0:
+            far_buffer[i] = block.astype(BF16)
+            sent.append(send(far_buffer.at[i], far_refs[i], out_sems.at[i]))
         else:
-            far_refs[i - len(near)][...] = block.astype(BF16)
+            share(block, me_ref[0] % 2, keep_ref, near_buffer, n)
+            sent.append(send(near_buffer.at[n], send_ref.at[n], out_sems.at[i]))
+    for copy in sent:
+        copy.wait()
 
 
 def share_kernel(me_ref, *refs):
@@ -190,12 +199,17 @@
         out_ref[2 * q + 1] = b.astype(BF16).reshape(shape)
 
 
-def inverse_kernel(came_ref, table_ref, out_ref, *, scale):
-    left, right = swap_halves(came_ref[:, 0].astype(F32), came_ref[:, 1].astype(F32), 1)
-    rows = left.shape[0] * 8
-    data = jnp.concatenate([left.reshape(rows, LANES), right.reshape(rows, LANES)], axis=1).astype(BF16)
-    out = lax.dot_general(data, table_ref[...], (((0,), (0,)), ((), ())), preferred_element_type=F32)
-    out_ref[...] = out * scale
+def inverse_kernel(came_ref, table_ref, out_ref, buffer, sems, *, scale):
+    halves = swap_halves(came_ref[:, 0].astype(F32), came_ref[:, 1].astype(F32), 1)
+    sent = []
+    for i, half in enumerate(halves):
+        data = half.reshape(half.shape[0] * 8, LANES).astype(BF16)
+        out = lax.dot_general(data, table_ref[...], (((0,), (0,)), ((), ())), preferred_element_type=F32)
+        at = pl.ds(i * LANES, LANES)
+        buffer[at] = out * scale
+        sent.append(send(buffer.at[at], out_ref.at[at], sems.at[i]))
+    for copy in sent:
+        copy.wait()
 
 
 def along_z(z, s, steps, sign=1):
@@ -231,7 +245,14 @@
         place,
         green,
         specs=[SMEM, ANY],
-        scratch_shapes=[pltpu.VMEM((steps, k_block, 2 * v_sub, x_cells), F32), pltpu.SemaphoreType.DMA((steps,))],
+        results=(VMEM, ANY) + (ANY,) * len(far),
+        scratch_shapes=[
+            pltpu.VMEM((steps, k_block, 2 * v_sub, x_cells), F32),
+            pltpu.VMEM(shared.shape, BF16),
+            pltpu.VMEM((len(far), 2 * rows, x_cells), BF16),
+            pltpu.SemaphoreType.DMA((steps,)),
+            pltpu.SemaphoreType.DMA((steps,)),
+        ],
     )
     came_near = swap_y(send_near)
     inward = [shift_z(piece, s) for piece, s in zip(outward, far)]
@@ -276,7 +297,8 @@
         array(lines, y_cells, dtype=F32),
         back.reshape(y_cells // 8, 2, 8, LANES),
         table,
-        keep=False,
+        results=ANY,
+        scratch_shapes=[pltpu.VMEM((lines, y_cells), F32), pltpu.SemaphoreType.DMA((lines // LANES,))],
     )
     return out.reshape(z_slab, x_local, y_cells)
 

time: 101 us -> 101 us (level)
  no operation moved by 1% of the time
where the time goes in v2:
time: 101 us
  starting transfers between devices  33.9 us (34%)
  blocking collectives  32.9 us (33%)
  waiting for transfers between devices  20.5 us (20%)
  Pallas kernels  11.7 us (12%)
  local copies, waits for them, and re-layouts  1.75 us (2%)
    all_to_all x1, blocking collectives, local(): lax.all_to_all(solved.reshape(pencils * groups, 8, LANES), ('pa', 'gz'),...  32.9 us
    ppermute x7, waiting for transfers between devices, shift_z(): return lax.ppermute(piece, 'gz', pairs)  20.5 us
    ppermute x7, starting transfers between devices, shift_z(): return lax.ppermute(piece, 'gz', pairs)  16.8 us
    all_to_all x1, starting transfers between devices, local(): lax.all_to_all(forward.reshape(pencils * groups, 8, LANES), ('pa', 'gz'),...  15.6 us
    pallas_call x8, Pallas kernels, call(): pl.pallas_call(kernel, out_shape=outs, in_specs=specs, out_specs=results,...  11.7 us
  transfers between devices with their start and end apart: 10, of which 4 were waited for; matrix products, arithmetic and copies ran while one was open for 0% of the time, Pallas kernels for 5%

profile of v2, /device:TPU:1, one launch (start us, length us, event | category | flops | bytes accessed | tf_op | source)
XLA Modules:
  0.0 100.9 jit_solution(13037247396725006841)
XLA Ops:
  0.0 0.0 copy-start
  0.0 1.0 %copy-done = bf16[4,64,1024]{2,1,0:T(8,128)(2,1)S(1)} copy-done((bf16[4,64,1024]{2,1,0:T(8,128)(2,1)S(1)}, bf16[4,64,1024]{2,1,0:T(8,128)(2,1)}, u32[]{:S(2)}) %copy-start) | copy-done | bytes 524312
  1.0 2.3 %shard_map.28 = (bf16[128,2,8,128]{3,2,1,0:T(8,128)(2,1)}, bf16[1024,1024]{1,0:T(8,128)(2,1)S(1)}) custom-call(bf16[256,1024]{1,0:T(8,128)(2,1)S(1)} %bitcast.10), custom_call_target="tpu_custom_call" | custom-call | tf_op jit(solution)/shard_map/pallas_call | solution.py:24
  3.3 15.6 %all-to-all-start = ((bf16[256,8,128]{2,1,0:T(8,128)(2,1)}), bf16[256,8,128]{2,1,0:T(8,128)(2,1)S(1)}, u32[]{:S(2)}, u32[]{:S(2)}) async-start(bf16[256,8,128]{2,1,0:T(8,128)(2,1)} %bitcast.1), calls=%async_computation | async-start | bytes 1048576 | tf_op jit(solution)/shard_map/all_to_all | solution.py:268
  19.0 2.3 %shard_map.31 = (bf16[5,32,1024]{2,1,0:T(8,128)(2,1)S(1)}, bf16[5,32,1024]{2,1,0:T(8,128)(2,1)S(1)}, bf16[64,1024]{1,0:T(8,128)(2,1)S(1)}, bf16[64,1024]{1,0:T(8,128)(2,1)S(1)}, bf16[64,1024]{1,0:T(8,128)(2,1)S(1)}) custom-call(s32[1]{0:T(128)} %bitcast.3.refs_0_.me_ref, f32[8,64,1024]{2,1,0:T(8,128)} %refs_1_.1), custom_call_target="tpu_custom_call" | custom-call | tf_op jit(solution)/shard_map/pallas_call | solution.py:24
  21.2 1.4 %collective-permute-start = (bf16[5,32,1024]{2,1,0:T(8,128)(2,1)S(1)}, bf16[5,32,1024]{2,1,0:T(8,128)(2,1)S(1)}, u32[]{:S(2)}, u32[]{:S(2)}) collective-permute-start(bf16[5,32,1024]{2,1,0:T(8,128)(2,1)S(1)} %get-tuple-element.25), channel_id=1, source_target_pairs={{0,16},{16,0},{32,48},{48,32},{64,80},{80,64},{96,112},{112,96},{1... | collective-permute-start | bytes 983048 | tf_op jit(solution)/shard_map/ppermute | solution.py:238
  22.7 3.7 %collective-permute-start.5 = (bf16[64,1024]{1,0:T(8,128)(2,1)S(1)}, bf16[64,1024]{1,0:T(8,128)(2,1)S(1)}, u32[]{:S(2)}, u32[]{:S(2)}) collective-permute-start(bf16[64,1024]{1,0:T(8,128)(2,1)S(1)} %get-tuple-element.30), channel_id=1, source_target_pairs={{0,96},{16,112},{32,128},{48,144},{64,160},{80,176},{96,192},{112,... | collective-permute-start | bytes 393224 | tf_op jit(solution)/shard_map/ppermute | solution.py:235
  26.4 3.5 %collective-permute-start.6 = (bf16[64,1024]{1,0:T(8,128)(2,1)S(1)}, bf16[64,1024]{1,0:T(8,128)(2,1)S(1)}, u32[]{:S(2)}, u32[]{:S(2)}) collective-permute-start(bf16[64,1024]{1,0:T(8,128)(2,1)S(1)} %get-tuple-element.31), channel_id=1, source_target_pairs={{0,128},{16,144},{32,160},{48,176},{64,192},{80,208},{96,224},{112... | collective-permute-start | bytes 393224 | tf_op jit(solution)/shard_map/ppermute | solution.py:235
  29.9 3.4 %collective-permute-start.7 = (bf16[64,1024]{1,0:T(8,128)(2,1)S(1)}, bf16[64,1024]{1,0:T(8,128)(2,1)S(1)}, u32[]{:S(2)}, u32[]{:S(2)}) collective-permute-start(bf16[64,1024]{1,0:T(8,128)(2,1)S(1)} %get-tuple-element.32), channel_id=1, source_target_pairs={{0,160},{16,176},{32,192},{48,208},{64,224},{80,240},{96,0},{112,1... | collective-permute-start | bytes 393224 | tf_op jit(solution)/shard_map/ppermute | solution.py:235
  33.3 10.4 %collective-permute-done.5.refs_0_ = bf16[64,1024]{1,0:T(8,128)(2,1)S(1)} collective-permute-done((bf16[64,1024]{1,0:T(8,128)(2,1)S(1)}, bf16[64,1024]{1,0:T(8,128)(2,1)S(1)}, u32[]{:S(2)}, u32[]{:S(2)}) %collective-permute-start.5) | collective-permute-done | bytes 131104 | tf_op jit(solution)/shard_map/ppermute | solution.py:235
  43.6 5.9 %collective-permute-done.6.refs_1_ = bf16[64,1024]{1,0:T(8,128)(2,1)S(1)} collective-permute-done((bf16[64,1024]{1,0:T(8,128)(2,1)S(1)}, bf16[64,1024]{1,0:T(8,128)(2,1)S(1)}, u32[]{:S(2)}, u32[]{:S(2)}) %collective-permute-start.6) | collective-permute-done | bytes 131104 | tf_op jit(solution)/shard_map/ppermute | solution.py:235
  49.6 0.0 collective-permute-done.7.refs_2_
  49.6 0.8 shard_map.33
  50.4 0.0 copy-start.3
  50.4 0.0 collective-permute-start.8
  50.4 0.0 collective-permute-done.came_ref.refs_6_
  50.4 0.9 shard_map.32
  51.2 0.9 collective-permute-start.1
  52.2 1.8 %collective-permute-start.2 = (bf16[64,1024]{1,0:T(8,128)(2,1)}, bf16[64,1024]{1,0:T(8,128)(2,1)}, u32[]{:S(2)}, u32[]{:S(2)}) collective-permute-start(bf16[64,1024]{1,0:T(8,128)(2,1)} %get-tuple-element.27), channel_id=1, source_target_pairs={{0,224},{16,240},{32,0},{48,16},{64,32},{80,48},{96,64},{112,80},{... | collective-permute-start | bytes 393224 | tf_op jit(solution)/shard_map/ppermute | solution.py:235
  53.9 0.4 collective-permute-start.3
  54.3 3.1 %collective-permute-start.4 = (bf16[64,1024]{1,0:T(8,128)(2,1)}, bf16[64,1024]{1,0:T(8,128)(2,1)}, u32[]{:S(2)}, u32[]{:S(2)}) collective-permute-start(bf16[64,1024]{1,0:T(8,128)(2,1)} %get-tuple-element.29), channel_id=1, source_target_pairs={{0,192},{16,208},{32,224},{48,240},{64,0},{80,16},{96,32},{112,48}... | collective-permute-start | bytes 393224 | tf_op jit(solution)/shard_map/ppermute | solution.py:235
  57.5 0.0 copy-done.3
  57.5 0.7 shard_map.30
  58.2 0.0 copy-start.1
  58.2 0.7 copy-done.1
  58.9 0.0 all-to-all-done
  58.9 0.0 copy-start.2
  58.9 0.0 copy-start.4
  58.9 0.8 shard_map.29.spec_ref
  59.7 0.0 collective-permute-done.8.refs_7_
  59.7 0.0 collective-permute-done.1.refs_0_
  59.7 0.0 collective-permute-done.2.refs_1_
  59.7 1.6 %collective-permute-done.3.refs_2_ = bf16[64,1024]{1,0:T(8,128)(2,1)} collective-permute-done((bf16[64,1024]{1,0:T(8,128)(2,1)}, bf16[64,1024]{1,0:T(8,128)(2,1)}, u32[]{:S(2)}, u32[]{:S(2)}) %collective-permute-start.3) | collective-permute-done | bytes 131104 | tf_op jit(solution)/shard_map/ppermute | solution.py:235
  61.3 2.6 %collective-permute-done.4.refs_3_ = bf16[64,1024]{1,0:T(8,128)(2,1)} collective-permute-done((bf16[64,1024]{1,0:T(8,128)(2,1)}, bf16[64,1024]{1,0:T(8,128)(2,1)}, u32[]{:S(2)}, u32[]{:S(2)}) %collective-permute-start.4) | collective-permute-done | bytes 131104 | tf_op jit(solution)/shard_map/ppermute | solution.py:235
  63.9 0.0 copy-done.2
  63.9 0.0 copy-done.4
  63.9 2.5 %shard_map.34 = bf16[16,16,8,128]{3,2,1,0:T(8,128)(2,1)S(1)} custom-call(bf16[256,1024]{1,0:T(8,128)(2,1)S(1)} %shard_map.29.spec_ref, bf16[512,256]{1,0:T(8,128)(2,1)S(1)} %get-tuple-element.22.forth_ref, bf16[256,512]{1,0:T(8,128)(2,1)S(1)} %copy-done.2, bf16[1024,1024]{1,0:T(8,128)(2,1)S(1)} %get-tuple-element.21.table_ref.refs_1_, ...), custom_call_target="tpu_custom_call" | custom-call | tf_op jit(solution)/shard_map/pallas_call | solution.py:24
  66.4 32.9 %all_to_all.10 = bf16[256,8,128]{2,1,0:T(8,128)(2,1)S(1)} all-to-all(bf16[256,8,128]{2,1,0:T(8,128)(2,1)S(1)} %bitcast.7), channel_id=1, replica_groups=mesh['gz'=16,'pa'=16] {'pa','gz'}, dimensions={0} | all-to-all | bytes 1048576 | tf_op jit(solution)/shard_map/all_to_all | solution.py:291
  99.4 1.6 %shard_map.35 = f32[256,1024]{1,0:T(8,128)} custom-call(bf16[128,2,8,128]{3,2,1,0:T(8,128)(2,1)S(1)} %bitcast.8, bf16[1024,1024]{1,0:T(8,128)(2,1)S(1)} %get-tuple-element.21.table_ref.refs_1_), custom_call_target="tpu_custom_call" | custom-call | tf_op jit(solution)/shard_map/pallas_call | solution.py:24
Async XLA Ops:
  0.0 1.0 %copy-start = (bf16[4,64,1024]{2,1,0:T(8,128)(2,1)S(1)}, bf16[4,64,1024]{2,1,0:T(8,128)(2,1)}, u32[]{:S(2)}) copy-start(bf16[4,64,1024]{2,1,0:T(8,128)(2,1)} %param.2) | copy-start | bytes 1572868
  3.3 55.6 %all-to-all-start = ((bf16[256,8,128]{2,1,0:T(8,128)(2,1)}), bf16[256,8,128]{2,1,0:T(8,128)(2,1)S(1)}, u32[]{:S(2)}, u32[]{:S(2)}) async-start(bf16[256,8,128]{2,1,0:T(8,128)(2,1)} %bitcast.1), calls=%async_computation | async-start | bytes 1048576 | tf_op jit(solution)/shard_map/all_to_all | solution.py:268
  21.2 29.1 %collective-permute-start = (bf16[5,32,1024]{2,1,0:T(8,128)(2,1)S(1)}, bf16[5,32,1024]{2,1,0:T(8,128)(2,1)S(1)}, u32[]{:S(2)}, u32[]{:S(2)}) collective-permute-start(bf16[5,32,1024]{2,1,0:T(8,128)(2,1)S(1)} %get-tuple-element.25), channel_id=1, source_target_pairs={{0,16},{16,0},{32,48},{48,32},{64,80},{80,64},{96,112},{112,96},{1... | collective-permute-start | bytes 983048 | tf_op jit(solution)/shard_map/ppermute | solution.py:238
  22.7 20.9 %collective-permute-start.5 = (bf16[64,1024]{1,0:T(8,128)(2,1)S(1)}, bf16[64,1024]{1,0:T(8,128)(2,1)S(1)}, u32[]{:S(2)}, u32[]{:S(2)}) collective-permute-start(bf16[64,1024]{1,0:T(8,128)(2,1)S(1)} %get-tuple-element.30), channel_id=1, source_target_pairs={{0,96},{16,112},{32,128},{48,144},{64,160},{80,176},{96,192},{112,... | collective-permute-start | bytes 393224 | tf_op jit(solution)/shard_map/ppermute | solution.py:235
  26.4 23.2 %collective-permute-start.6 = (bf16[64,1024]{1,0:T(8,128)(2,1)S(1)}, bf16[64,1024]{1,0:T(8,128)(2,1)S(1)}, u32[]{:S(2)}, u32[]{:S(2)}) collective-permute-start(bf16[64,1024]{1,0:T(8,128)(2,1)S(1)} %get-tuple-element.31), channel_id=1, source_target_pairs={{0,128},{16,144},{32,160},{48,176},{64,192},{80,208},{96,224},{112... | collective-permute-start | bytes 393224 | tf_op jit(solution)/shard_map/ppermute | solution.py:235
  29.9 19.7 %collective-permute-start.7 = (bf16[64,1024]{1,0:T(8,128)(2,1)S(1)}, bf16[64,1024]{1,0:T(8,128)(2,1)S(1)}, u32[]{:S(2)}, u32[]{:S(2)}) collective-permute-start(bf16[64,1024]{1,0:T(8,128)(2,1)S(1)} %get-tuple-element.32), channel_id=1, source_target_pairs={{0,160},{16,176},{32,192},{48,208},{64,224},{80,240},{96,0},{112,1... | collective-permute-start | bytes 393224 | tf_op jit(solution)/shard_map/ppermute | solution.py:235
  50.4 7.1 %copy-start.3 = (bf16[3,32,1024]{2,1,0:T(8,128)(2,1)}, bf16[3,32,1024]{2,1,0:T(8,128)(2,1)S(1)}, u32[]{:S(2)}) copy-start(bf16[3,32,1024]{2,1,0:T(8,128)(2,1)S(1)} %get-tuple-element.33.refs_5_) | copy-start | bytes 589828
  50.4 9.3 %collective-permute-start.8 = (bf16[3,32,1024]{2,1,0:T(8,128)(2,1)}, bf16[3,32,1024]{2,1,0:T(8,128)(2,1)}, u32[]{:S(2)}, u32[]{:S(2)}) collective-permute-start(bf16[3,32,1024]{2,1,0:T(8,128)(2,1)} %get-tuple-element.34), channel_id=1, source_target_pairs={{0,16},{16,0},{32,48},{48,32},{64,80},{80,64},{96,112},{112,96},{1... | collective-permute-start | bytes 589832 | tf_op jit(solution)/shard_map/ppermute | solution.py:238
  51.2 8.5 %collective-permute-start.1 = (bf16[64,1024]{1,0:T(8,128)(2,1)}, bf16[64,1024]{1,0:T(8,128)(2,1)}, u32[]{:S(2)}, u32[]{:S(2)}) collective-permute-start(bf16[64,1024]{1,0:T(8,128)(2,1)} %get-tuple-element.26), channel_id=1, source_target_pairs={{0,32},{16,48},{32,64},{48,80},{64,96},{80,112},{96,128},{112,144}... | collective-permute-start | bytes 393224 | tf_op jit(solution)/shard_map/ppermute | solution.py:235
  52.2 7.6 %collective-permute-start.2 = (bf16[64,1024]{1,0:T(8,128)(2,1)}, bf16[64,1024]{1,0:T(8,128)(2,1)}, u32[]{:S(2)}, u32[]{:S(2)}) collective-permute-start(bf16[64,1024]{1,0:T(8,128)(2,1)} %get-tuple-element.27), channel_id=1, source_target_pairs={{0,224},{16,240},{32,0},{48,16},{64,32},{80,48},{96,64},{112,80},{... | collective-permute-start | bytes 393224 | tf_op jit(solution)/shard_map/ppermute | solution.py:235
  53.9 7.4 %collective-permute-start.3 = (bf16[64,1024]{1,0:T(8,128)(2,1)}, bf16[64,1024]{1,0:T(8,128)(2,1)}, u32[]{:S(2)}, u32[]{:S(2)}) collective-permute-start(bf16[64,1024]{1,0:T(8,128)(2,1)} %get-tuple-element.28), channel_id=1, source_target_pairs={{0,64},{16,80},{32,96},{48,112},{64,128},{80,144},{96,160},{112,17... | collective-permute-start | bytes 393224 | tf_op jit(solution)/shard_map/ppermute | solution.py:235
  54.3 9.5 %collective-permute-start.4 = (bf16[64,1024]{1,0:T(8,128)(2,1)}, bf16[64,1024]{1,0:T(8,128)(2,1)}, u32[]{:S(2)}, u32[]{:S(2)}) collective-permute-start(bf16[64,1024]{1,0:T(8,128)(2,1)} %get-tuple-element.29), channel_id=1, source_target_pairs={{0,192},{16,208},{32,224},{48,240},{64,0},{80,16},{96,32},{112,48}... | collective-permute-start | bytes 393224 | tf_op jit(solution)/shard_map/ppermute | solution.py:235
  58.2 0.7 copy-start.1
  58.9 5.0 %copy-start.2 = (bf16[256,512]{1,0:T(8,128)(2,1)S(1)}, bf16[256,512]{1,0:T(8,128)(2,1)}, u32[]{:S(2)}) copy-start(bf16[256,512]{1,0:T(8,128)(2,1)} %copy-done.1) | copy-start | bytes 786436
  58.9 5.0 %copy-start.4 = (bf16[3,32,1024]{2,1,0:T(8,128)(2,1)S(1)}, bf16[3,32,1024]{2,1,0:T(8,128)(2,1)}, u32[]{:S(2)}) copy-start(bf16[3,32,1024]{2,1,0:T(8,128)(2,1)} %copy-done.3) | copy-start | bytes 589828

commit v3 on v2

--- a/solution.py
+++ b/solution.py
@@ -151,15 +151,23 @@
     back_ref[...] = jnp.where(same, full, 0.0).astype(BF16)
 
 
-def forward_kernel(density_ref, out_ref, table_ref):
+def forward_kernel(density_ref, out_ref, table_ref, buffer, sems):
     cas_square(table_ref)
     spec = lax.dot_general(table_ref[...], density_ref[...], (((1,), (1,)), ((), ())), preferred_element_type=F32)
-    tiles = spec.shape[0] // 8
-    left = spec[:, :LANES].reshape(tiles, 8, LANES)
-    right = spec[:, LANES:].reshape(tiles, 8, LANES)
-    even, odd = swap_halves(left, right, 1)
-    out_ref[:, 0] = even.astype(BF16)
-    out_ref[:, 1] = odd.astype(BF16)
+    chunks = sems.shape[0]
+    tiles = spec.shape[0] // 8 // chunks
+    sent = []
+    for c in range(chunks):
+        part = spec[c * tiles * 8 : (c + 1) * tiles * 8]
+        left = part[:, :LANES].reshape(tiles, 8, LANES)
+        right = part[:, LANES:].reshape(tiles, 8, LANES)
+        even, odd = swap_halves(left, right, 1)
+        at = pl.ds(c * tiles, tiles)
+        buffer[at, 0] = even.astype(BF16)
+        buffer[at, 1] = odd.astype(BF16)
+        sent.append(send(buffer.at[at], out_ref.at[at], sems.at[c]))
+    for copy in sent:
+        copy.wait()
 
 
 def spectrum_kernel(moved_ref, table_ref, out_ref):
@@ -257,13 +265,17 @@
     came_near = swap_y(send_near)
     inward = [shift_z(piece, s) for piece, s in zip(outward, far)]
     shared = array(len(far), rows, x_cells)
-    keep_far, send_far = call(share_kernel, (shared, shared), place, *inward, specs=[SMEM] + [VMEM] * len(far))
+    keep_far, send_far = call(share_kernel, (pltpu.HBM(shared.shape, BF16),) * 2, place, *inward, specs=[SMEM] + [VMEM] * len(far))
     came_far = swap_y(send_far)
     pieces = call(join_kernel, (array(2 * rows, x_cells),) * (len(near) - 1), keep_near, came_near)
     pieces = [shift_z(piece, s) for piece, s in zip(pieces, near[1:])]
 
     forward, table = call(
-        forward_kernel, (array(y_cells // 8, 2, 8, LANES), array(y_cells, y_cells)), density.reshape(lines, y_cells)
+        forward_kernel,
+        (pltpu.HBM((y_cells // 8, 2, 8, LANES), BF16), array(y_cells, y_cells)),
+        density.reshape(lines, y_cells),
+        results=(ANY, VMEM),
+        scratch_shapes=[pltpu.VMEM((y_cells // 8, 2, 8, LANES), BF16), pltpu.SemaphoreType.DMA((4,))],
     )
     moved = lax.all_to_all(
         forward.reshape(pencils * groups, 8, LANES), ("pa", "gz"), split_axis=0, concat_axis=0, tiled=True
@@ -271,7 +283,7 @@
     spectrum = call(spectrum_kernel, array(groups * 16, x_cells), moved.reshape(pencils, groups, 8, LANES), table)
     forth, inverse_z = call(
         lambda *refs: expand_kernel(*refs, order=order, groups=groups, v_sub=v_sub, k_block=k_block, z_slab=z_slab),
-        (array(z_freqs * v_sub, groups * 16), array(groups * 16, z_freqs * v_sub)),
+        (pltpu.HBM((z_freqs * v_sub, groups * 16), BF16), pltpu.HBM((groups * 16, z_freqs * v_sub), BF16)),
         place,
         specs=[SMEM],
     )

time: 101 us -> 101 us (level)
  transfers between devices with their start and end apart: 10 -> 10, of which waited for: 4 -> 4; matrix products, arithmetic and copies ran while one was open for 0% -> 0% of each run, Pallas kernels for 5% -> 6%
where the time goes in v3:
time: 101 us
  starting transfers between devices  33.9 us (34%)
  blocking collectives  32.9 us (33%)
  waiting for transfers between devices  20.5 us (20%)
  Pallas kernels  12.5 us (12%)
  local copies, waits for them, and re-layouts  1.05 us (1%)
    all_to_all x1, blocking collectives, local(): lax.all_to_all(solved.reshape(pencils * groups, 8, LANES), ('pa', 'gz'),...  32.9 us
    ppermute x7, waiting for transfers between devices, shift_z(): return lax.ppermute(piece, 'gz', pairs)  20.5 us
    ppermute x7, starting transfers between devices, shift_z(): return lax.ppermute(piece, 'gz', pairs)  16.8 us
    all_to_all x1, starting transfers between devices, local(): lax.all_to_all(forward.reshape(pencils * groups, 8, LANES), ('pa', 'gz'),...  15.7 us
    pallas_call x8, Pallas kernels, call(): pl.pallas_call(kernel, out_shape=outs, in_specs=specs, out_specs=results,...  12.5 us
  transfers between devices with their start and end apart: 10, of which 4 were waited for; matrix products, arithmetic and copies ran while one was open for 0% of the time, Pallas kernels for 6%

profile of v3, /device:TPU:1, one launch (start us, length us, event | category | flops | bytes accessed | tf_op | source)
XLA Modules:
  0.0 100.9 jit_solution(106210149153718481)
XLA Ops:
  0.0 0.0 copy-start
  0.0 1.0 %copy-done = bf16[4,64,1024]{2,1,0:T(8,128)(2,1)S(1)} copy-done((bf16[4,64,1024]{2,1,0:T(8,128)(2,1)S(1)}, bf16[4,64,1024]{2,1,0:T(8,128)(2,1)}, u32[]{:S(2)}) %copy-start) | copy-done | bytes 524312
  1.0 2.2 %shard_map.28 = (bf16[128,2,8,128]{3,2,1,0:T(8,128)(2,1)}, bf16[1024,1024]{1,0:T(8,128)(2,1)S(1)}) custom-call(bf16[256,1024]{1,0:T(8,128)(2,1)S(1)} %bitcast.10), custom_call_target="tpu_custom_call" | custom-call | tf_op jit(solution)/shard_map/pallas_call | solution.py:24
  3.2 15.7 %all-to-all-start = ((bf16[256,8,128]{2,1,0:T(8,128)(2,1)}), bf16[256,8,128]{2,1,0:T(8,128)(2,1)S(1)}, u32[]{:S(2)}, u32[]{:S(2)}) async-start(bf16[256,8,128]{2,1,0:T(8,128)(2,1)} %bitcast.11), calls=%async_computation | async-start | bytes 1048576 | tf_op jit(solution)/shard_map/all_to_all | solution.py:280
  18.9 2.3 %shard_map.31 = (bf16[5,32,1024]{2,1,0:T(8,128)(2,1)S(1)}, bf16[5,32,1024]{2,1,0:T(8,128)(2,1)S(1)}, bf16[64,1024]{1,0:T(8,128)(2,1)S(1)}, bf16[64,1024]{1,0:T(8,128)(2,1)S(1)}, bf16[64,1024]{1,0:T(8,128)(2,1)S(1)}) custom-call(s32[1]{0:T(128)} %bitcast.3.refs_0_.me_ref, f32[8,64,1024]{2,1,0:T(8,128)} %refs_1_.1), custom_call_target="tpu_custom_call" | custom-call | tf_op jit(solution)/shard_map/pallas_call | solution.py:24
  21.2 1.4 %collective-permute-start = (bf16[5,32,1024]{2,1,0:T(8,128)(2,1)S(1)}, bf16[5,32,1024]{2,1,0:T(8,128)(2,1)S(1)}, u32[]{:S(2)}, u32[]{:S(2)}) collective-permute-start(bf16[5,32,1024]{2,1,0:T(8,128)(2,1)S(1)} %get-tuple-element.25), channel_id=1, source_target_pairs={{0,16},{16,0},{32,48},{48,32},{64,80},{80,64},{96,112},{112,96},{1... | collective-permute-start | bytes 983048 | tf_op jit(solution)/shard_map/ppermute | solution.py:246
  22.6 3.7 %collective-permute-start.5 = (bf16[64,1024]{1,0:T(8,128)(2,1)S(1)}, bf16[64,1024]{1,0:T(8,128)(2,1)S(1)}, u32[]{:S(2)}, u32[]{:S(2)}) collective-permute-start(bf16[64,1024]{1,0:T(8,128)(2,1)S(1)} %get-tuple-element.30), channel_id=1, source_target_pairs={{0,96},{16,112},{32,128},{48,144},{64,160},{80,176},{96,192},{112,... | collective-permute-start | bytes 393224 | tf_op jit(solution)/shard_map/ppermute | solution.py:243
  26.3 3.5 %collective-permute-start.6 = (bf16[64,1024]{1,0:T(8,128)(2,1)S(1)}, bf16[64,1024]{1,0:T(8,128)(2,1)S(1)}, u32[]{:S(2)}, u32[]{:S(2)}) collective-permute-start(bf16[64,1024]{1,0:T(8,128)(2,1)S(1)} %get-tuple-element.31), channel_id=1, source_target_pairs={{0,128},{16,144},{32,160},{48,176},{64,192},{80,208},{96,224},{112... | collective-permute-start | bytes 393224 | tf_op jit(solution)/shard_map/ppermute | solution.py:243
  29.8 3.4 %collective-permute-start.7 = (bf16[64,1024]{1,0:T(8,128)(2,1)S(1)}, bf16[64,1024]{1,0:T(8,128)(2,1)S(1)}, u32[]{:S(2)}, u32[]{:S(2)}) collective-permute-start(bf16[64,1024]{1,0:T(8,128)(2,1)S(1)} %get-tuple-element.32), channel_id=1, source_target_pairs={{0,160},{16,176},{32,192},{48,208},{64,224},{80,240},{96,0},{112,1... | collective-permute-start | bytes 393224 | tf_op jit(solution)/shard_map/ppermute | solution.py:243
  33.2 10.4 %collective-permute-done.5.refs_0_ = bf16[64,1024]{1,0:T(8,128)(2,1)S(1)} collective-permute-done((bf16[64,1024]{1,0:T(8,128)(2,1)S(1)}, bf16[64,1024]{1,0:T(8,128)(2,1)S(1)}, u32[]{:S(2)}, u32[]{:S(2)}) %collective-permute-start.5) | collective-permute-done | bytes 131104 | tf_op jit(solution)/shard_map/ppermute | solution.py:243
  43.6 5.9 %collective-permute-done.6.refs_1_ = bf16[64,1024]{1,0:T(8,128)(2,1)S(1)} collective-permute-done((bf16[64,1024]{1,0:T(8,128)(2,1)S(1)}, bf16[64,1024]{1,0:T(8,128)(2,1)S(1)}, u32[]{:S(2)}, u32[]{:S(2)}) %collective-permute-start.6) | collective-permute-done | bytes 131104 | tf_op jit(solution)/shard_map/ppermute | solution.py:243
  49.5 0.0 collective-permute-done.7.refs_2_
  49.5 0.9 shard_map.33
  50.4 0.0 collective-permute-start.8
  50.4 0.0 collective-permute-done.came_ref.refs_6_
  50.4 0.8 shard_map.32
  51.2 0.9 collective-permute-start.1
  52.2 1.7 %collective-permute-start.2 = (bf16[64,1024]{1,0:T(8,128)(2,1)}, bf16[64,1024]{1,0:T(8,128)(2,1)}, u32[]{:S(2)}, u32[]{:S(2)}) collective-permute-start(bf16[64,1024]{1,0:T(8,128)(2,1)} %get-tuple-element.27), channel_id=1, source_target_pairs={{0,224},{16,240},{32,0},{48,16},{64,32},{80,48},{96,64},{112,80},{... | collective-permute-start | bytes 393224 | tf_op jit(solution)/shard_map/ppermute | solution.py:243
  53.9 0.5 collective-permute-start.3
  54.4 3.1 %collective-permute-start.4 = (bf16[64,1024]{1,0:T(8,128)(2,1)}, bf16[64,1024]{1,0:T(8,128)(2,1)}, u32[]{:S(2)}, u32[]{:S(2)}) collective-permute-start(bf16[64,1024]{1,0:T(8,128)(2,1)} %get-tuple-element.29), channel_id=1, source_target_pairs={{0,192},{16,208},{32,224},{48,240},{64,0},{80,16},{96,32},{112,48}... | collective-permute-start | bytes 393224 | tf_op jit(solution)/shard_map/ppermute | solution.py:243
  57.5 1.5 %shard_map.30 = (bf16[512,256]{1,0:T(8,128)(2,1)}, bf16[256,512]{1,0:T(8,128)(2,1)}) custom-call(s32[1]{0:T(128)} %bitcast.3.refs_0_.me_ref), custom_call_target="tpu_custom_call" | custom-call | tf_op jit(solution)/shard_map/pallas_call | solution.py:24
  58.9 0.0 copy-start.1
  58.9 0.0 all-to-all-done
  58.9 0.0 copy-start.2
  58.9 0.0 copy-start.3
  59.0 0.8 shard_map.29.spec_ref
  59.7 0.0 collective-permute-done.8.refs_7_
  59.7 0.0 collective-permute-done.1.refs_0_
  59.7 0.0 collective-permute-done.2.refs_1_
  59.8 1.5 %collective-permute-done.3.refs_2_ = bf16[64,1024]{1,0:T(8,128)(2,1)} collective-permute-done((bf16[64,1024]{1,0:T(8,128)(2,1)}, bf16[64,1024]{1,0:T(8,128)(2,1)}, u32[]{:S(2)}, u32[]{:S(2)}) %collective-permute-start.3) | collective-permute-done | bytes 131104 | tf_op jit(solution)/shard_map/ppermute | solution.py:243
  61.3 2.6 %collective-permute-done.4.refs_3_ = bf16[64,1024]{1,0:T(8,128)(2,1)} collective-permute-done((bf16[64,1024]{1,0:T(8,128)(2,1)}, bf16[64,1024]{1,0:T(8,128)(2,1)}, u32[]{:S(2)}, u32[]{:S(2)}) %collective-permute-start.4) | collective-permute-done | bytes 131104 | tf_op jit(solution)/shard_map/ppermute | solution.py:243
  63.9 0.0 copy-done.1
  63.9 0.0 copy-done.2
  63.9 0.0 copy-done.3
  63.9 2.5 %shard_map.34 = bf16[16,16,8,128]{3,2,1,0:T(8,128)(2,1)S(1)} custom-call(bf16[256,1024]{1,0:T(8,128)(2,1)S(1)} %shard_map.29.spec_ref, bf16[512,256]{1,0:T(8,128)(2,1)S(1)} %copy-done.1, bf16[256,512]{1,0:T(8,128)(2,1)S(1)} %copy-done.2, bf16[1024,1024]{1,0:T(8,128)(2,1)S(1)} %get-tuple-element.21.table_ref.refs_1_, ...), custom_call_target="tpu_custom_call" | custom-call | tf_op jit(solution)/shard_map/pallas_call | solution.py:24
  66.4 32.9 %all_to_all.10 = bf16[256,8,128]{2,1,0:T(8,128)(2,1)S(1)} all-to-all(bf16[256,8,128]{2,1,0:T(8,128)(2,1)S(1)} %bitcast.7), channel_id=1, replica_groups=mesh['gz'=16,'pa'=16] {'pa','gz'}, dimensions={0} | all-to-all | bytes 1048576 | tf_op jit(solution)/shard_map/all_to_all | solution.py:303
  99.4 1.6 %shard_map.35 = f32[256,1024]{1,0:T(8,128)} custom-call(bf16[128,2,8,128]{3,2,1,0:T(8,128)(2,1)S(1)} %bitcast.8, bf16[1024,1024]{1,0:T(8,128)(2,1)S(1)} %get-tuple-element.21.table_ref.refs_1_), custom_call_target="tpu_custom_call" | custom-call | tf_op jit(solution)/shard_map/pallas_call | solution.py:24
Async XLA Ops:
  0.0 1.0 %copy-start = (bf16[4,64,1024]{2,1,0:T(8,128)(2,1)S(1)}, bf16[4,64,1024]{2,1,0:T(8,128)(2,1)}, u32[]{:S(2)}) copy-start(bf16[4,64,1024]{2,1,0:T(8,128)(2,1)} %param.2) | copy-start | bytes 1572868
  3.2 55.7 %all-to-all-start = ((bf16[256,8,128]{2,1,0:T(8,128)(2,1)}), bf16[256,8,128]{2,1,0:T(8,128)(2,1)S(1)}, u32[]{:S(2)}, u32[]{:S(2)}) async-start(bf16[256,8,128]{2,1,0:T(8,128)(2,1)} %bitcast.11), calls=%async_computation | async-start | bytes 1048576 | tf_op jit(solution)/shard_map/all_to_all | solution.py:280
  21.2 29.2 %collective-permute-start = (bf16[5,32,1024]{2,1,0:T(8,128)(2,1)S(1)}, bf16[5,32,1024]{2,1,0:T(8,128)(2,1)S(1)}, u32[]{:S(2)}, u32[]{:S(2)}) collective-permute-start(bf16[5,32,1024]{2,1,0:T(8,128)(2,1)S(1)} %get-tuple-element.25), channel_id=1, source_target_pairs={{0,16},{16,0},{32,48},{48,32},{64,80},{80,64},{96,112},{112,96},{1... | collective-permute-start | bytes 983048 | tf_op jit(solution)/shard_map/ppermute | solution.py:246
  22.6 20.9 %collective-permute-start.5 = (bf16[64,1024]{1,0:T(8,128)(2,1)S(1)}, bf16[64,1024]{1,0:T(8,128)(2,1)S(1)}, u32[]{:S(2)}, u32[]{:S(2)}) collective-permute-start(bf16[64,1024]{1,0:T(8,128)(2,1)S(1)} %get-tuple-element.30), channel_id=1, source_target_pairs={{0,96},{16,112},{32,128},{48,144},{64,160},{80,176},{96,192},{112,... | collective-permute-start | bytes 393224 | tf_op jit(solution)/shard_map/ppermute | solution.py:243
  26.3 23.2 %collective-permute-start.6 = (bf16[64,1024]{1,0:T(8,128)(2,1)S(1)}, bf16[64,1024]{1,0:T(8,128)(2,1)S(1)}, u32[]{:S(2)}, u32[]{:S(2)}) collective-permute-start(bf16[64,1024]{1,0:T(8,128)(2,1)S(1)} %get-tuple-element.31), channel_id=1, source_target_pairs={{0,128},{16,144},{32,160},{48,176},{64,192},{80,208},{96,224},{112... | collective-permute-start | bytes 393224 | tf_op jit(solution)/shard_map/ppermute | solution.py:243
  29.8 19.7 %collective-permute-start.7 = (bf16[64,1024]{1,0:T(8,128)(2,1)S(1)}, bf16[64,1024]{1,0:T(8,128)(2,1)S(1)}, u32[]{:S(2)}, u32[]{:S(2)}) collective-permute-start(bf16[64,1024]{1,0:T(8,128)(2,1)S(1)} %get-tuple-element.32), channel_id=1, source_target_pairs={{0,160},{16,176},{32,192},{48,208},{64,224},{80,240},{96,0},{112,1... | collective-permute-start | bytes 393224 | tf_op jit(solution)/shard_map/ppermute | solution.py:243
  50.4 9.3 %collective-permute-start.8 = (bf16[3,32,1024]{2,1,0:T(8,128)(2,1)}, bf16[3,32,1024]{2,1,0:T(8,128)(2,1)}, u32[]{:S(2)}, u32[]{:S(2)}) collective-permute-start(bf16[3,32,1024]{2,1,0:T(8,128)(2,1)} %get-tuple-element.34), channel_id=1, source_target_pairs={{0,16},{16,0},{32,48},{48,32},{64,80},{80,64},{96,112},{112,96},{1... | collective-permute-start | bytes 589832 | tf_op jit(solution)/shard_map/ppermute | solution.py:246
  51.2 8.5 %collective-permute-start.1 = (bf16[64,1024]{1,0:T(8,128)(2,1)}, bf16[64,1024]{1,0:T(8,128)(2,1)}, u32[]{:S(2)}, u32[]{:S(2)}) collective-permute-start(bf16[64,1024]{1,0:T(8,128)(2,1)} %get-tuple-element.26), channel_id=1, source_target_pairs={{0,32},{16,48},{32,64},{48,80},{64,96},{80,112},{96,128},{112,144}... | collective-permute-start | bytes 393224 | tf_op jit(solution)/shard_map/ppermute | solution.py:243
  52.2 7.6 %collective-permute-start.2 = (bf16[64,1024]{1,0:T(8,128)(2,1)}, bf16[64,1024]{1,0:T(8,128)(2,1)}, u32[]{:S(2)}, u32[]{:S(2)}) collective-permute-start(bf16[64,1024]{1,0:T(8,128)(2,1)} %get-tuple-element.27), channel_id=1, source_target_pairs={{0,224},{16,240},{32,0},{48,16},{64,32},{80,48},{96,64},{112,80},{... | collective-permute-start | bytes 393224 | tf_op jit(solution)/shard_map/ppermute | solution.py:243
  53.9 7.4 %collective-permute-start.3 = (bf16[64,1024]{1,0:T(8,128)(2,1)}, bf16[64,1024]{1,0:T(8,128)(2,1)}, u32[]{:S(2)}, u32[]{:S(2)}) collective-permute-start(bf16[64,1024]{1,0:T(8,128)(2,1)} %get-tuple-element.28), channel_id=1, source_target_pairs={{0,64},{16,80},{32,96},{48,112},{64,128},{80,144},{96,160},{112,17... | collective-permute-start | bytes 393224 | tf_op jit(solution)/shard_map/ppermute | solution.py:243
  54.4 9.5 %collective-permute-start.4 = (bf16[64,1024]{1,0:T(8,128)(2,1)}, bf16[64,1024]{1,0:T(8,128)(2,1)}, u32[]{:S(2)}, u32[]{:S(2)}) collective-permute-start(bf16[64,1024]{1,0:T(8,128)(2,1)} %get-tuple-element.29), channel_id=1, source_target_pairs={{0,192},{16,208},{32,224},{48,240},{64,0},{80,16},{96,32},{112,48}... | collective-permute-start | bytes 393224 | tf_op jit(solution)/shard_map/ppermute | solution.py:243
  58.9 5.0 %copy-start.1 = (bf16[512,256]{1,0:T(8,128)(2,1)S(1)}, bf16[512,256]{1,0:T(8,128)(2,1)}, u32[]{:S(2)}) copy-start(bf16[512,256]{1,0:T(8,128)(2,1)} %get-tuple-element.22.forth_ref) | copy-start | bytes 786436
  58.9 5.0 %copy-start.2 = (bf16[256,512]{1,0:T(8,128)(2,1)S(1)}, bf16[256,512]{1,0:T(8,128)(2,1)}, u32[]{:S(2)}) copy-start(bf16[256,512]{1,0:T(8,128)(2,1)} %get-tuple-element.23.back_ref) | copy-start | bytes 786436
  58.9 5.0 %copy-start.3 = (bf16[3,32,1024]{2,1,0:T(8,128)(2,1)S(1)}, bf16[3,32,1024]{2,1,0:T(8,128)(2,1)}, u32[]{:S(2)}) copy-start(bf16[3,32,1024]{2,1,0:T(8,128)(2,1)} %get-tuple-element.33.refs_5_) | copy-start | bytes 589828
